TPU v7x, 32 devices: a whole 2x2x4 slice. The times are simulated.
32 devices in a mesh: groups: 2 (over y), fld: 8 (over z, x), rep: 2 (over core).
Axes of the slice: x: 2, y: 2, z: 4, core: 2. Of those that a mesh axis runs over, the one named last changes fastest.
Arguments:
- feature_ids: int32 [4096, 40], P('groups', 'fld'), parts along dimension 0, may hold values from 0 to 65535, as said below
- field_slot: int32 [40], replicated, may hold values from 0 to 39, as said below
- table: bfloat16 [2621440, 64], P(('fld', 'rep')), may hold values from -48 to 48
- query_weight: bfloat16 [2, 64, 64], replicated, may hold values from -0.75 to 0.75
- key_weight: bfloat16 [2, 64, 64], replicated, may hold values from -0.75 to 0.75
- value_weight: bfloat16 [2, 64, 64], replicated, may hold values from -0.75 to 0.75
- residual_weight: bfloat16 [2, 64, 64], replicated, may hold values from -0.75 to 0.75
- out_weight: float32 [40, 64], replicated, may hold values from -0.125 to 0.125
Outputs:
- interacted: bfloat16 [40, 4096, 64], P('fld', ('groups', 'rep')), parts along dimension 1
- logits: float32 [2, 2048], P('rep', ('groups', 'fld')), parts along dimension 1
There are 2 independent parts, one for each index of `groups`. A program takes and returns all parts, laid end to end along the dimension named above; an argument that names none is the same for every part. Nothing has to cross between parts.
Inputs may be any that keep to these rules, and one draw needn't show every extreme that they name: `feature_ids`: in each column the ids lie below a table size of that slot, which differs from slot to slot. `field_slot`: distinct slots.
All inputs are finite; a program needn't handle non-finite values.
Results may differ from a plain program's by a relative error of at most 0.006.
The roundings to bfloat16 on the way count: a program that leaves them out, or rounds other values in their place, can miss the bound.
Values may be sent and summed in bfloat16 or wider, within the bound.
No kernel may reach another device: no remote copies, remote signals or barrier semaphores. Data moves between devices by JAX's collectives and lax.ppermute only.
A program may use at most 128 MiB of HBM per device.

v0:
```python
import functools
import math

import jax
import jax.numpy as jnp
from jax import lax
from jax.experimental import pallas as pl
from jax.experimental.pallas import tpu as pltpu
from jax.sharding import PartitionSpec as P

HEADS = 2
F32 = jnp.float32
BF16 = jnp.bfloat16
LANES = 128
VMEM_BYTES = 58 * 1024 * 1024


def divisor(count, options):
    return next(c for c in options if count % c == 0)


def by_rep(options):
    rep = lax.axis_index("rep")
    found = jnp.int32(options[0])
    for r, option in enumerate(options[1:], 1):
        found = jnp.where(rep == r, jnp.int32(option), found)
    return found


def lookup_kernel(
    ids_ref, tab_ref, *refs, step, slot_of, shift_of, bounds_of, owned
):
    out_ref, land, tab, stage, lines, odd_ref, row_ref, sem, row_sem = refs[-9:]
    blocks, slots, width, lanes = out_ref.shape
    reps = len(bounds_of[0])
    rep = lax.axis_index("rep")
    buffers = land.shape[0]
    batch = stage.shape[0] // lanes
    spare = tab.shape[0] - 8
    bounds = [by_rep(b) for b in bounds_of]
    first, last = bounds[0], bounds[-1]
    pairs = step // (2 * lanes)

    def fetch(c):
        b = lax.rem(c, buffers)
        at = pl.ds(pl.multiple_of(c * step, step), step)
        return pltpu.make_async_copy(tab_ref.at[:, at], land.at[b], sem.at[b])

    for i in range(buffers):

        @pl.when(first + i < last)
        def _():
            fetch(first + i).start()

    tab[pl.ds(spare, 8), :] = jnp.zeros((8, 2 * width), F32)
    for j in range(slots):
        shift = by_rep(shift_of[j])
        for b in range(blocks):
            at = ((b % reps) * (blocks // reps) + b // reps) * lanes
            rows = ids_ref[slot_of[j][0] : slot_of[j][0] + 1, at : at + lanes]
            for r, slot in enumerate(slot_of[j][1:], 1):
                rows = jnp.where(rep == r, ids_ref[slot : slot + 1, at : at + lanes], rows)
            rows = rows + shift
            here = (rows >= 0) & (rows < owned)
            rows = rows - first * step
            line = ((rows >> 8) << 7) | (rows & (lanes - 1))
            lines[pl.ds(j * blocks + b, 1), :] = jnp.where(here, line, spare)
            odd_ref[pl.ds(j * blocks + b, 1), :] = (rows >> 7) & 1
    rows_copy = pltpu.make_async_copy(lines, row_ref, row_sem)
    rows_copy.start()
    rows_copy.wait()
    for j in range(slots):

        def chunk(c, carry):
            fetch(c).wait()
            b = lax.rem(c, buffers)

            def turn(p, carry):
                at = pl.multiple_of(p * (2 * lanes), 2 * lanes)
                two = jnp.concatenate(
                    [land[b, :, pl.ds(at, lanes)], land[b, :, pl.ds(at + lanes, lanes)]], axis=0
                )
                to = pl.multiple_of((c - first) * (step // 2) + p * lanes, lanes)
                tab[pl.ds(to, lanes), :] = two.T.astype(F32)
                return carry

            lax.fori_loop(0, pairs, turn, 0, unroll=min(pairs, 64))

            @pl.when(c + buffers < last)
            def _():
                fetch(c + buffers).start()

            return carry

        lax.fori_loop(bounds[j], bounds[j + 1], chunk, 0)

        def some_blocks(i, carry, j=j):
            def some(n, carry):
                at = j * blocks + i * batch + n
                to = n * lanes
                for u in range(lanes):
                    stage[pl.ds(to + u, 1), :] = tab[pl.ds(row_ref[at, u], 1), :]
                return carry

            lax.fori_loop(0, batch, some, 0)
            for g in range(batch):
                b = i * batch + g
                turned = stage[g * lanes : (g + 1) * lanes].astype(BF16).T.astype(F32)
                odd = odd_ref[pl.ds(j * blocks + b, 1), :] > 0
                out_ref[b, j] = jnp.where(odd, turned[width:], turned[:width]).astype(BF16)
            return carry

        lax.fori_loop(0, blocks // batch, some_blocks, 0)


def lookup(ids, table_t, blocks, slot_of, shift_of, bounds_of, step, most):
    width, owned = table_t.shape
    slots = len(slot_of)
    buffers = min(4, owned // step)
    batch = divisor(blocks, (4, 2, 1))
    vmem = pl.BlockSpec(memory_space=pltpu.VMEM)
    anywhere = pl.BlockSpec(memory_space=pl.ANY)
    return pl.pallas_call(
        functools.partial(
            lookup_kernel,
            step=step,
            slot_of=slot_of,
            shift_of=shift_of,
            bounds_of=bounds_of,
            owned=owned,
        ),
        out_shape=jax.ShapeDtypeStruct((blocks, slots, width, LANES), BF16),
        in_specs=[vmem, anywhere],
        out_specs=vmem,
        scratch_shapes=[
            pltpu.VMEM((buffers, width, step), BF16),
            pltpu.VMEM((most // 2 + 8, 2 * width), F32),
            pltpu.VMEM((batch * LANES, 2 * width), F32),
            pltpu.VMEM((slots * blocks, LANES), jnp.int32),
            pltpu.VMEM((slots * blocks, LANES), jnp.int32),
            pltpu.SMEM((slots * blocks, LANES), jnp.int32),
            pltpu.SemaphoreType.DMA((buffers,)),
            pltpu.SemaphoreType.DMA,
        ],
        compiler_params=pltpu.CompilerParams(vmem_limit_bytes=VMEM_BYTES),
        cost_estimate=pl.CostEstimate(
            flops=slots * 12_000_000_000, bytes_accessed=2 * most * width, transcendentals=0
        ),
    )(ids, table_t)


def project(load, w, q_s, k_s, v_s, r_s, fields, width, lanes):
    def pair(i, carry):
        f = 2 * i
        x2 = jnp.concatenate([load(f), load(f + 1)], axis=1)
        y = lax.dot_general(w, x2, (((1,), (0,)), ((), ())), preferred_element_type=F32)
        for u in range(2):
            yu = y[:, u * lanes : (u + 1) * lanes]
            qkv = yu[: 3 * width].astype(BF16).astype(F32)
            q_s[f + u] = qkv[:width]
            k_s[pl.ds(f + u, width, stride=fields), :] = qkv[width : 2 * width]
            v_s[f + u] = qkv[2 * width :]
            r_s[f + u] = yu[3 * width :]
        return carry

    lax.fori_loop(0, fields // 2, pair, 0)


def attend(q_s, k_s, v_s, r_s, a_s, store, field_of, count, fields, width, group):
    size = width // HEADS
    scale = math.log2(math.e) / math.sqrt(size)

    def some(i, carry):
        own = [field_of(i * group + u) for u in range(group)]
        for h in range(HEADS):
            scores = [None] * group
            for d in range(size):
                row = h * size + d
                match = k_s[row * fields : (row + 1) * fields, :]
                for u in range(group):
                    term = match * q_s[own[u], pl.ds(row, 1), :]
                    scores[u] = term if scores[u] is None else scores[u] + term
            for u in range(group):
                top = jnp.max(scores[u], axis=0, keepdims=True)
                e = jnp.exp2((scores[u] - top) * scale)
                total = jnp.sum(e, axis=0, keepdims=True)
                a_s[u * fields : (u + 1) * fields, :] = (e / total).astype(BF16).astype(F32)
            mixed = [None] * group
            for g in range(fields):
                content = v_s[g, h * size : (h + 1) * size, :]
                for u in range(group):
                    term = content * a_s[u * fields + g : u * fields + g + 1, :]
                    mixed[u] = term if mixed[u] is None else mixed[u] + term
            for u in range(group):
                out = mixed[u] + r_s[own[u], h * size : (h + 1) * size, :]
                store(i * group + u, h * size, jnp.maximum(out, 0.0).astype(BF16))
        return carry

    lax.fori_loop(0, count // group, some, 0)


def layer_weights(refs, l):
    return jnp.concatenate([ref[l].astype(F32).T.astype(BF16) for ref in refs], axis=0)


def interact_kernel(place_ref, wq_ref, wk_ref, wv_ref, wr_ref, *refs, cuts, sources, group, part, opens):
    count = len(cuts) if opens else 1
    in_refs, o_ref = refs[:count], refs[count]
    refs = refs[count + 1 :]
    q_s, k_s, v_s, r_s, a_s = refs[-5:]
    chips, out_slots, width, lanes = o_ref.shape
    fields = q_s.shape[0]
    layers = wq_ref.shape[0]
    size = width // HEADS
    per = len(sources)
    whole = chips * per == fields
    weights = (wq_ref, wk_ref, wv_ref, wr_ref)

    if opens:
        x_s, h_s = refs[-6], refs[0]

        def gather(i, carry):
            for local, parts in enumerate(sources):
                found = None
                for r, j in parts:
                    cut = next(n for n, (low, high) in enumerate(cuts) if low <= j < high)
                    piece = in_refs[cut][i, r, j - cuts[cut][0]]
                    found = piece if found is None else found + piece
                x_s[i * per + local] = found
            return carry

        lax.fori_loop(0, chips, gather, 0)
    else:
        h_s = in_refs[0]

    for l in range(0 if opens else layers - 1, layers):
        if l == 0:
            load = lambda f: x_s[f if whole else place_ref[f]]
        else:
            load = lambda f: h_s[f]
        project(load, layer_weights(weights, l), q_s, k_s, v_s, r_s, fields, width, lanes)
        if l < layers - 1:

            def store(f, at, out):
                h_s[f, at : at + size, :] = out

            attend(q_s, k_s, v_s, r_s, a_s, store, lambda f: f, fields, fields, width, group)
        elif whole:

            def store(n, at, out):
                o_ref[lax.rem(n, chips), lax.div(n, chips), at : at + size, :] = out

            def field_of(n):
                return lax.rem(n, chips) * per + lax.div(n, chips) + part[0]

            total = chips * out_slots
            attend(q_s, k_s, v_s, r_s, a_s, store, field_of, total, fields, width, group)
        else:

            def clear(i, carry):
                for local in range(out_slots):
                    o_ref[i, local] = jnp.zeros((width, lanes), BF16)
                return carry

            lax.fori_loop(0, chips, clear, 0)

            def store(f, at, out):
                slot = place_ref[f]
                o_ref[lax.div(slot, per), lax.rem(slot, per), at : at + size, :] = out

            attend(q_s, k_s, v_s, r_s, a_s, store, lambda f: f, fields, fields, width, group)


def interact(place, given, chips, cuts, weights, sources, fields, part, opens, more):
    width, lanes = given[0].shape[-2:]
    group = divisor(fields, (4, 2, 1))
    wide = pltpu.VMEM((fields, width, lanes), F32)
    vmem = pl.BlockSpec(memory_space=pltpu.VMEM)
    layer_in = jax.ShapeDtypeStruct((fields, width, lanes), BF16)
    outs = [jax.ShapeDtypeStruct((chips, part[1] - part[0], width, lanes), BF16)]
    scratch = [
        wide,
        pltpu.VMEM((width * fields, lanes), F32),
        wide,
        wide,
        pltpu.VMEM((group * fields, lanes), F32),
    ]
    if opens:
        scratch = [pltpu.VMEM((chips * len(sources), width, lanes), BF16)] + scratch
        if more:
            outs.append(layer_in)
        else:
            scratch = [pltpu.VMEM((fields, width, lanes), BF16)] + scratch
    return pl.pallas_call(
        functools.partial(
            interact_kernel, cuts=tuple(cuts), sources=sources, group=group, part=part, opens=opens
        ),
        out_shape=outs,
        in_specs=[pl.BlockSpec(memory_space=pltpu.SMEM)] + [vmem] * (4 + len(given)),
        out_specs=[vmem] * len(outs),
        scratch_shapes=scratch,
        compiler_params=pltpu.CompilerParams(vmem_limit_bytes=VMEM_BYTES),
        cost_estimate=pl.CostEstimate(
            flops=12_000_000_000, bytes_accessed=4_000_000, transcendentals=0
        ),
    )(place, *weights, *given)


def per_device(
    feature_ids,
    field_slot,
    table,
    query_weight,
    key_weight,
    value_weight,
    residual_weight,
    out_weight,
):
    total, per = feature_ids.shape
    owned, width = table.shape
    chips = lax.axis_size("fld")
    reps = lax.axis_size("rep")
    half = total // reps
    peer = half // chips
    blocks = chips * reps
    rows_slot = owned * reps // per
    slot_count = chips * per
    fields = field_slot.shape[0]

    spans = [(r * owned // rows_slot, -(-(r + 1) * owned // rows_slot)) for r in range(reps)]
    held = max(b - a for a, b in spans)
    held_slots = [[min(a, per - held) + j for j in range(held)] for a, _ in spans]
    sources = tuple(
        tuple((r, held_slots[r].index(s)) for r in range(reps) if spans[r][0] <= s < spans[r][1])
        for s in range(per)
    )
    step = divisor(owned, (16384, 8192, 4096, 2048, 1024, 512, 256))
    slot_ids = jnp.transpose(feature_ids)
    table_t = jnp.transpose(table)
    ranks = range(reps)

    def look_up(low, high):
        shift_of = [
            [(held_slots[r][j]) * rows_slot - r * owned for r in ranks] for j in range(low, high)
        ]
        starts = [max(0, shift_of[0][r]) // step for r in ranks]
        bounds_of = [starts] + [
            [max(starts[r], min(owned // step, -(-(shift[r] + rows_slot) // step))) for r in ranks]
            for shift in shift_of
        ]
        most = max(end - start for end, start in zip(bounds_of[-1], starts)) * step
        slot_of = [[held_slots[r][j] for r in ranks] for j in range(low, high)]
        return lookup(slot_ids, table_t, blocks, slot_of, shift_of, bounds_of, step, most)

    def exchange(found):
        arrived = lax.all_to_all(found, ("fld", "rep"), 0, 0, tiled=True)
        return arrived.reshape(chips, reps, found.shape[1], width, peer)

    cuts = [(0, held)]
    founds = []
    for cut in cuts:
        founds.append(look_up(*cut))
    arrived = []
    for found in founds:
        arrived.append(exchange(found))
    weights = (query_weight, key_weight, value_weight, residual_weight)

    parts = parts_of(per)
    given = arrived
    hidden, sent = [], []
    for n, part in enumerate(parts):
        more = n + 1 < len(parts)
        done = interact(
            field_slot, given, chips, cuts, weights, sources, fields, part, n == 0, more
        )
        hidden.append(done[0])
        given = done[1:] if n == 0 else given
    for block in hidden:
        sent.append(lax.all_to_all(block, "fld", 0, 0, tiled=True))
    select = (field_slot[:, None] == jnp.arange(slot_count, dtype=jnp.int32)[None, :]).astype(F32)
    slot_weight = jnp.einsum("fs,fd->sd", select, out_weight, precision=lax.Precision.HIGHEST)
    slot_weight = slot_weight.reshape(chips, per, width)
    logits = sum(
        jnp.einsum(
            "csdn,csd->n",
            block.astype(F32),
            slot_weight[:, low:high],
            precision=lax.Precision.HIGHEST,
        )
        for block, (low, high) in zip(hidden, parts)
    )
    interacted = jnp.concatenate(
        [x.transpose(1, 0, 3, 2).reshape(x.shape[1], half, width) for x in sent], axis=0
    )
    return (interacted, logits.reshape(1, peer))


def parts_of(per):
    return [(0, per)]


def solution(mesh):
    placed = (P("groups", "fld"), P(), P(("fld", "rep"), None), P(), P(), P(), P(), P())

    return jax.shard_map(
        per_device,
        mesh=mesh,
        in_specs=placed,
        out_specs=(P("fld", ("groups", "rep"), None), P("rep", ("groups", "fld"))),
        check_vma=False,
    )
```

profile of v0, /device:TPU:0, one launch (start us, length us, event | category | flops | bytes accessed | tf_op | source)
XLA Modules:
  0.0 91.8 jit_solution(7872510237862129)
XLA Ops:
  0.6 0.0 copy-start
  0.6 15.6 %shard_map.95 = bf16[16,3,64,128]{3,2,1,0:T(8,128)(2,1)} custom-call(s32[5,2048]{1,0:T(8,128)} %bitcast.21, bf16[64,163840]{1,0:T(8,128)(2,1)} %bitcast.20), custom_call_target="tpu_custom_call" | custom-call | flops 35999997952 | bytes 20971520 | tf_op jit(solution)/shard_map/pallas_call | solution.py:123
  16.2 27.6 %all_to_all.10 = bf16[16,3,64,128]{3,2,1,0:T(8,128)(2,1)} all-to-all(bf16[16,3,64,128]{3,2,1,0:T(8,128)(2,1)} %shard_map.95), channel_id=1, replica_groups=mesh['groups'=2,'fld'=8,'rep'=2] {'fld','rep'}, dimensions={0} | all-to-all | bytes 1572864 | tf_op jit(solution)/shard_map/all_to_all | solution.py:356
  43.8 0.0 copy-start.1
  43.8 24.8 %shard_map.96 = bf16[8,5,64,128]{3,2,1,0:T(8,128)(2,1)} custom-call(s32[40]{0:T(128)} %place_ref.1, bf16[2,64,64]{2,1,0:T(8,128)(2,1)} %wq_ref.1, bf16[2,64,64]{2,1,0:T(8,128)(2,1)} %wk_ref.1, bf16[2,64,64]{2,1,0:T(8,128)(2,1)} %wv_ref.1, bf16[2,64,64]{2,1,0:T(8,128)(2,1)} %wr_ref.1, bf16[8,2,3,64,128]{4,3,2,1,0:T(8,128)(2,1)} %bitcast.19), custom_call_target="tpu_custom_call" | custom-call | flops 12000000000 | bytes 4000000 | tf_op jit(solution)/shard_map/pallas_call | solution.py:294
  68.7 3.8 %all-to-all-start.1 = ((bf16[8,5,64,128]{3,2,1,0:T(8,128)(2,1)}), bf16[8,5,64,128]{3,2,1,0:T(8,128)(2,1)S(1)}, u32[]{:S(2)}, u32[]{:S(2)}) async-start(bf16[8,5,64,128]{3,2,1,0:T(8,128)(2,1)} %shard_map.96), calls=%async_computation.1 | async-start | bytes 1310720 | tf_op jit(solution)/shard_map/all_to_all | solution.py:379
  72.5 0.0 copy-done
  72.5 0.0 copy-done.1
  72.5 0.3 fusion
  72.8 2.0 %convolution_bitcast_fusion = f32[1,128]{1,0:T(1,128)} fusion(bf16[8,5,64,128]{3,2,1,0:T(8,128)(2,1)} %shard_map.96, f32[8,5,64,1]{2,3,1,0:T(1,128)S(1)} %bitcast.22), kind=kOutput, calls=%fused_computation | convolution fusion | flops 3932160 | bytes 666112 | tf_op jit(solution)/shard_map/csdn,csd->n/dot_general | solution.py:384
  74.8 16.0 %all-to-all-done.1 = bf16[8,5,64,128]{3,2,1,0:T(8,128)(2,1)S(1)} async-done(((bf16[8,5,64,128]{3,2,1,0:T(8,128)(2,1)}), bf16[8,5,64,128]{3,2,1,0:T(8,128)(2,1)S(1)}, u32[]{:S(2)}, u32[]{:S(2)}) %all-to-all-start.1) | async-done | bytes 655392 | tf_op jit(solution)/shard_map/all_to_all | solution.py:379
  90.8 0.9 %copy_bitcast_fusion = bf16[5,1024,64]{1,2,0:T(8,128)(2,1)} fusion(bf16[8,5,64,128]{3,2,1,0:T(8,128)(2,1)S(1)} %all-to-all-done.1), kind=kLoop, calls=%fused_computation.1 | loop fusion | bytes 1310720 | tf_op jit(solution)/shard_map/reshape | solution.py:393
Async XLA Ops:
  0.6 71.9 %copy-start = (f32[40,64]{1,0:T(8,128)S(1)}, f32[40,64]{1,0:T(8,128)}, u32[]{:S(2)}) copy-start(f32[40,64]{1,0:T(8,128)} %param.15) | copy-start | bytes 30724
  43.8 28.7 %copy-start.1 = (s32[40]{0:T(128)S(1)}, s32[40]{0:T(128)}, u32[]{:S(2)}) copy-start(s32[40]{0:T(128)} %place_ref.1) | copy-start | bytes 484
  68.7 22.2 %all-to-all-start.1 = ((bf16[8,5,64,128]{3,2,1,0:T(8,128)(2,1)}), bf16[8,5,64,128]{3,2,1,0:T(8,128)(2,1)S(1)}, u32[]{:S(2)}, u32[]{:S(2)}) async-start(bf16[8,5,64,128]{3,2,1,0:T(8,128)(2,1)} %shard_map.96), calls=%async_computation.1 | async-start | bytes 1310720 | tf_op jit(solution)/shard_map/all_to_all | solution.py:379
where the time goes:
time: 92.2 us; the launch traced here: 91.8 us
  Pallas kernels  40.4 us (44%)
  blocking collectives  27.6 us (30%)
  waiting for transfers between devices  16 us (17%)
  starting transfers between devices  3.83 us (4%)
  matrix products  2.31 us (3%)
  local copies, waits for them, and re-layouts  0.95 us (1%)
    all_to_all x1, blocking collectives, exchange(): arrived = lax.all_to_all(found, ('fld', 'rep'), 0, 0, tiled=True)  27.6 us
    pallas_call x1, Pallas kernels, interact(): pl.pallas_call(functools.partial(interact_kernel, cuts=tuple(cuts), sourc...  24.8 us
    all_to_all x1, waiting for transfers between devices, per_device(): sent.append(lax.all_to_all(block, 'fld', 0, 0, tiled=True))  16 us
    pallas_call x1, Pallas kernels, lookup(): pl.pallas_call(functools.partial(lookup_kernel, step=step, slot_of=slot_o...  15.6 us
    all_to_all x1, starting transfers between devices, per_device(): sent.append(lax.all_to_all(block, 'fld', 0, 0, tiled=True))  3.83 us
    dot_general x1, matrix products, per_device(): jnp.einsum('csdn,csd->n', block.astype(F32), slot_weight[:, low:high], pr...  2.03 us
  transfers between devices with their start and end apart: 1, of which 1 were waited for; matrix products, arithmetic and copies ran while one was open for 3% of the time, Pallas kernels for 0%

commit v1 on v0

--- a/solution.py
+++ b/solution.py
@@ -149,50 +149,96 @@
     )(ids, table_t)
 
 
-def project(load, w, q_s, k_s, v_s, r_s, fields, width, lanes):
+ROWS = 8
+CHAINS = 4
+
+
+def project(load, w, q_s, kt_s, k_s, v_s, r_s):
+    fields, width, lanes = q_s.shape
+
     def pair(i, carry):
         f = 2 * i
         x2 = jnp.concatenate([load(f), load(f + 1)], axis=1)
         y = lax.dot_general(w, x2, (((1,), (0,)), ((), ())), preferred_element_type=F32)
+        ys = [y[:, :lanes], y[:, lanes:]]
         for u in range(2):
-            yu = y[:, u * lanes : (u + 1) * lanes]
-            qkv = yu[: 3 * width].astype(BF16).astype(F32)
-            q_s[f + u] = qkv[:width]
-            k_s[pl.ds(f + u, width, stride=fields), :] = qkv[width : 2 * width]
-            v_s[f + u] = qkv[2 * width :]
-            r_s[f + u] = yu[3 * width :]
+            q_s[f + u] = ys[u][:width]
+            kt_s[pl.ds(f + u, width, stride=fields), :] = ys[u][width : 2 * width]
+            r_s[f + u] = ys[u][3 * width :]
+        for t in range(width // ROWS):
+            at = 2 * width + ROWS * t
+            two = jnp.concatenate([yu[at : at + ROWS] for yu in ys], axis=0)
+            v_s[i, 2 * ROWS * t : 2 * ROWS * (t + 1)] = two.astype(BF16)
         return carry
 
-    lax.fori_loop(0, fields // 2, pair, 0)
-
-
-def attend(q_s, k_s, v_s, r_s, a_s, store, field_of, count, fields, width, group):
+    lax.fori_loop(0, fields // 2, pair, 0, unroll=divisor(fields // 2, (10, 8, 5, 4, 2, 1)))
+
+    def turn(i, carry):
+        rows = [
+            kt_s[pl.ds(pl.multiple_of((2 * i + u) * fields, ROWS), fields), :] for u in range(2)
+        ]
+        for t in range(fields // ROWS):
+            two = jnp.concatenate([x[ROWS * t : ROWS * (t + 1)] for x in rows], axis=0)
+            k_s[i, 2 * ROWS * t : 2 * ROWS * (t + 1)] = two.astype(BF16)
+        return carry
+
+    lax.fori_loop(0, width // 2, turn, 0, unroll=4)
+
+
+def spread(a, b):
+    shape = (ROWS, a.shape[1])
+    two = jnp.concatenate([jnp.broadcast_to(a, shape), jnp.broadcast_to(b, shape)], axis=0)
+    return two.astype(BF16).astype(F32)
+
+
+def halves(x):
+    return x[:ROWS] + x[ROWS:]
+
+
+def attend(q_s, k_s, v_s, r_s, a_s, store, field_of, count, group):
+    fields, width, _ = q_s.shape
     size = width // HEADS
     scale = math.log2(math.e) / math.sqrt(size)
+    tiles = fields // ROWS
+    whole = tiles // CHAINS * CHAINS
+    jobs = [
+        [(u, t) for t in range(n, n + CHAINS)] for n in range(0, whole, CHAINS) for u in range(group)
+    ]
+    left = [(u, t) for t in range(whole, tiles) for u in range(group)]
+    jobs += [left[n : n + CHAINS] for n in range(0, len(left), CHAINS)]
 
     def some(i, carry):
         own = [field_of(i * group + u) for u in range(group)]
         for h in range(HEADS):
-            scores = [None] * group
-            for d in range(size):
-                row = h * size + d
-                match = k_s[row * fields : (row + 1) * fields, :]
-                for u in range(group):
-                    term = match * q_s[own[u], pl.ds(row, 1), :]
-                    scores[u] = term if scores[u] is None else scores[u] + term
+            scores = {}
+            for job in jobs:
+                sums = {}
+                for d in range(h * size, (h + 1) * size, 2):
+                    qs = {
+                        u: spread(q_s[own[u], pl.ds(d, 1), :], q_s[own[u], pl.ds(d + 1, 1), :])
+                        for u, _ in job
+                    }
+                    for u, t in job:
+                        match = k_s[d // 2, 2 * ROWS * t : 2 * ROWS * (t + 1), :].astype(F32)
+                        term = match * qs[u]
+                        sums[u, t] = sums[u, t] + term if (u, t) in sums else term
+                scores.update((key, halves(x)) for key, x in sums.items())
             for u in range(group):
-                top = jnp.max(scores[u], axis=0, keepdims=True)
-                e = jnp.exp2((scores[u] - top) * scale)
-                total = jnp.sum(e, axis=0, keepdims=True)
-                a_s[u * fields : (u + 1) * fields, :] = (e / total).astype(BF16).astype(F32)
-            mixed = [None] * group
-            for g in range(fields):
-                content = v_s[g, h * size : (h + 1) * size, :]
-                for u in range(group):
-                    term = content * a_s[u * fields + g : u * fields + g + 1, :]
-                    mixed[u] = term if mixed[u] is None else mixed[u] + term
+                score = jnp.concatenate([scores[u, t] for t in range(tiles)], axis=0)
+                top = jnp.max(score, axis=0, keepdims=True)
+                e = jnp.exp2((score - top) * scale)
+                a_s[u * fields : (u + 1) * fields, :] = e / jnp.sum(e, axis=0, keepdims=True)
             for u in range(group):
-                out = mixed[u] + r_s[own[u], h * size : (h + 1) * size, :]
+                sums = {}
+                for g in range(0, fields, 2):
+                    at = u * fields + g
+                    weight = spread(a_s[at : at + 1, :], a_s[at + 1 : at + 2, :])
+                    for t in range(h * size // ROWS, (h + 1) * size // ROWS):
+                        content = v_s[g // 2, 2 * ROWS * t : 2 * ROWS * (t + 1), :].astype(F32)
+                        term = content * weight
+                        sums[t] = sums[t] + term if t in sums else term
+                mixed = jnp.concatenate([halves(x) for x in sums.values()], axis=0)
+                out = mixed + r_s[own[u], h * size : (h + 1) * size, :]
                 store(i * group + u, h * size, jnp.maximum(out, 0.0).astype(BF16))
         return carry
 
@@ -207,7 +253,7 @@
     count = len(cuts) if opens else 1
     in_refs, o_ref = refs[:count], refs[count]
     refs = refs[count + 1 :]
-    q_s, k_s, v_s, r_s, a_s = refs[-5:]
+    q_s, kt_s, k_s, v_s, r_s, a_s = refs[-6:]
     chips, out_slots, width, lanes = o_ref.shape
     fields = q_s.shape[0]
     layers = wq_ref.shape[0]
@@ -217,7 +263,7 @@
     weights = (wq_ref, wk_ref, wv_ref, wr_ref)
 
     if opens:
-        x_s, h_s = refs[-6], refs[0]
+        x_s, h_s = refs[-7], refs[0]
 
         def gather(i, carry):
             for local, parts in enumerate(sources):
@@ -238,13 +284,13 @@
             load = lambda f: x_s[f if whole else place_ref[f]]
         else:
             load = lambda f: h_s[f]
-        project(load, layer_weights(weights, l), q_s, k_s, v_s, r_s, fields, width, lanes)
+        project(load, layer_weights(weights, l), q_s, kt_s, k_s, v_s, r_s)
         if l < layers - 1:
 
             def store(f, at, out):
                 h_s[f, at : at + size, :] = out
 
-            attend(q_s, k_s, v_s, r_s, a_s, store, lambda f: f, fields, fields, width, group)
+            attend(q_s, k_s, v_s, r_s, a_s, store, lambda f: f, fields, group)
         elif whole:
 
             def store(n, at, out):
@@ -254,7 +300,7 @@
                 return lax.rem(n, chips) * per + lax.div(n, chips) + part[0]
 
             total = chips * out_slots
-            attend(q_s, k_s, v_s, r_s, a_s, store, field_of, total, fields, width, group)
+            attend(q_s, k_s, v_s, r_s, a_s, store, field_of, total, group)
         else:
 
             def clear(i, carry):
@@ -268,7 +314,7 @@
                 slot = place_ref[f]
                 o_ref[lax.div(slot, per), lax.rem(slot, per), at : at + size, :] = out
 
-            attend(q_s, k_s, v_s, r_s, a_s, store, lambda f: f, fields, fields, width, group)
+            attend(q_s, k_s, v_s, r_s, a_s, store, lambda f: f, fields, group)
 
 
 def interact(place, given, chips, cuts, weights, sources, fields, part, opens, more):
@@ -281,7 +327,8 @@
     scratch = [
         wide,
         pltpu.VMEM((width * fields, lanes), F32),
-        wide,
+        pltpu.VMEM((width // 2, 2 * fields, lanes), BF16),
+        pltpu.VMEM((fields // 2, 2 * width, lanes), BF16),
         wide,
         pltpu.VMEM((group * fields, lanes), F32),
     ]

time: 92.2 us -> 80.6 us (0.87)
  Pallas kernels: 40.4 us -> 28.8 us
    pallas_call x1, Pallas kernels: 24.8 us -> 13.2 us  [interact(): pl.pallas_call(functools.partial(interact_kernel, cuts=tuple(cuts), sourc...]
where the time goes in v1:
time: 80.6 us; the launch traced here: 80.2 us
  Pallas kernels  28.8 us (36%)
  blocking collectives  27.6 us (34%)
  waiting for transfers between devices  16 us (20%)
  starting transfers between devices  3.83 us (5%)
  matrix products  2.31 us (3%)
  local copies, waits for them, and re-layouts  0.95 us (1%)
    all_to_all x1, blocking collectives, exchange(): arrived = lax.all_to_all(found, ('fld', 'rep'), 0, 0, tiled=True)  27.6 us
    all_to_all x1, waiting for transfers between devices, per_device(): sent.append(lax.all_to_all(block, 'fld', 0, 0, tiled=True))  16 us
    pallas_call x1, Pallas kernels, lookup(): pl.pallas_call(functools.partial(lookup_kernel, step=step, slot_of=slot_o...  15.6 us
    pallas_call x1, Pallas kernels, interact(): pl.pallas_call(functools.partial(interact_kernel, cuts=tuple(cuts), sourc...  13.2 us
    all_to_all x1, starting transfers between devices, per_device(): sent.append(lax.all_to_all(block, 'fld', 0, 0, tiled=True))  3.83 us
    dot_general x1, matrix products, per_device(): jnp.einsum('csdn,csd->n', block.astype(F32), slot_weight[:, low:high], pr...  2.03 us
  transfers between devices with their start and end apart: 1, of which 1 were waited for; matrix products, arithmetic and copies ran while one was open for 3% of the time, Pallas kernels for 0%

profile of v1, /device:TPU:0, one launch (start us, length us, event | category | flops | bytes accessed | tf_op | source)
XLA Modules:
  0.0 80.2 jit_solution(10772340596705385753)
XLA Ops:
  0.6 0.0 copy-start
  0.6 15.6 %shard_map.95 = bf16[16,3,64,128]{3,2,1,0:T(8,128)(2,1)} custom-call(s32[5,2048]{1,0:T(8,128)} %bitcast.21, bf16[64,163840]{1,0:T(8,128)(2,1)} %bitcast.20), custom_call_target="tpu_custom_call" | custom-call | flops 35999997952 | bytes 20971520 | tf_op jit(solution)/shard_map/pallas_call | solution.py:123
  16.2 27.6 %all_to_all.10 = bf16[16,3,64,128]{3,2,1,0:T(8,128)(2,1)} all-to-all(bf16[16,3,64,128]{3,2,1,0:T(8,128)(2,1)} %shard_map.95), channel_id=1, replica_groups=mesh['groups'=2,'fld'=8,'rep'=2] {'fld','rep'}, dimensions={0} | all-to-all | bytes 1572864 | tf_op jit(solution)/shard_map/all_to_all | solution.py:403
  43.8 0.0 copy-start.1
  43.8 13.2 %shard_map.96 = bf16[8,5,64,128]{3,2,1,0:T(8,128)(2,1)} custom-call(s32[40]{0:T(128)} %place_ref.1, bf16[2,64,64]{2,1,0:T(8,128)(2,1)} %wq_ref.1, bf16[2,64,64]{2,1,0:T(8,128)(2,1)} %wk_ref.1, bf16[2,64,64]{2,1,0:T(8,128)(2,1)} %wv_ref.1, bf16[2,64,64]{2,1,0:T(8,128)(2,1)} %wr_ref.1, bf16[8,2,3,64,128]{4,3,2,1,0:T(8,128)(2,1)} %bitcast.19), custom_call_target="tpu_custom_call" | custom-call | flops 12000000000 | bytes 4000000 | tf_op jit(solution)/shard_map/pallas_call | solution.py:341
  57.1 3.8 %all-to-all-start.1 = ((bf16[8,5,64,128]{3,2,1,0:T(8,128)(2,1)}), bf16[8,5,64,128]{3,2,1,0:T(8,128)(2,1)S(1)}, u32[]{:S(2)}, u32[]{:S(2)}) async-start(bf16[8,5,64,128]{3,2,1,0:T(8,128)(2,1)} %shard_map.96), calls=%async_computation.1 | async-start | bytes 1310720 | tf_op jit(solution)/shard_map/all_to_all | solution.py:426
  60.9 0.0 copy-done
  60.9 0.0 copy-done.1
  60.9 0.3 fusion
  61.2 2.0 %convolution_bitcast_fusion = f32[1,128]{1,0:T(1,128)} fusion(bf16[8,5,64,128]{3,2,1,0:T(8,128)(2,1)} %shard_map.96, f32[8,5,64,1]{2,3,1,0:T(1,128)S(1)} %bitcast.22), kind=kOutput, calls=%fused_computation | convolution fusion | flops 3932160 | bytes 666112 | tf_op jit(solution)/shard_map/csdn,csd->n/dot_general | solution.py:431
  63.2 16.0 %all-to-all-done.1 = bf16[8,5,64,128]{3,2,1,0:T(8,128)(2,1)S(1)} async-done(((bf16[8,5,64,128]{3,2,1,0:T(8,128)(2,1)}), bf16[8,5,64,128]{3,2,1,0:T(8,128)(2,1)S(1)}, u32[]{:S(2)}, u32[]{:S(2)}) %all-to-all-start.1) | async-done | bytes 655392 | tf_op jit(solution)/shard_map/all_to_all | solution.py:426
  79.3 0.9 %copy_bitcast_fusion = bf16[5,1024,64]{1,2,0:T(8,128)(2,1)} fusion(bf16[8,5,64,128]{3,2,1,0:T(8,128)(2,1)S(1)} %all-to-all-done.1), kind=kLoop, calls=%fused_computation.1 | loop fusion | bytes 1310720 | tf_op jit(solution)/shard_map/reshape | solution.py:440
Async XLA Ops:
  0.6 60.3 %copy-start = (f32[40,64]{1,0:T(8,128)S(1)}, f32[40,64]{1,0:T(8,128)}, u32[]{:S(2)}) copy-start(f32[40,64]{1,0:T(8,128)} %param.15) | copy-start | bytes 30724
  43.8 17.1 %copy-start.1 = (s32[40]{0:T(128)S(1)}, s32[40]{0:T(128)}, u32[]{:S(2)}) copy-start(s32[40]{0:T(128)} %place_ref.1) | copy-start | bytes 484
  57.1 22.2 %all-to-all-start.1 = ((bf16[8,5,64,128]{3,2,1,0:T(8,128)(2,1)}), bf16[8,5,64,128]{3,2,1,0:T(8,128)(2,1)S(1)}, u32[]{:S(2)}, u32[]{:S(2)}) async-start(bf16[8,5,64,128]{3,2,1,0:T(8,128)(2,1)} %shard_map.96), calls=%async_computation.1 | async-start | bytes 1310720 | tf_op jit(solution)/shard_map/all_to_all | solution.py:426

commit v2 on v1

--- a/solution.py
+++ b/solution.py
@@ -30,9 +30,12 @@
 def lookup_kernel(
     ids_ref, tab_ref, *refs, step, slot_of, shift_of, bounds_of, owned
 ):
-    out_ref, land, tab, stage, lines, odd_ref, row_ref, sem, row_sem = refs[-9:]
-    blocks, slots, width, lanes = out_ref.shape
+    outs = refs[:-8]
+    land, tab, stage, lines, odd_ref, row_ref, sem, row_sem = refs[-8:]
+    chips, slots, width, lanes = outs[0].shape
     reps = len(bounds_of[0])
+    blocks = chips * reps
+    chip = lax.axis_index("fld")
     rep = lax.axis_index("rep")
     buffers = land.shape[0]
     batch = stage.shape[0] // lanes
@@ -56,10 +59,12 @@
     for j in range(slots):
         shift = by_rep(shift_of[j])
         for b in range(blocks):
-            at = ((b % reps) * (blocks // reps) + b // reps) * lanes
-            rows = ids_ref[slot_of[j][0] : slot_of[j][0] + 1, at : at + lanes]
+            to_rep = lax.rem(rep + b // chips, reps)
+            to_chip = lax.rem(chip + b % chips, chips)
+            at = pl.ds(pl.multiple_of((to_rep * chips + to_chip) * lanes, lanes), lanes)
+            rows = ids_ref[slot_of[j][0] : slot_of[j][0] + 1, at]
             for r, slot in enumerate(slot_of[j][1:], 1):
-                rows = jnp.where(rep == r, ids_ref[slot : slot + 1, at : at + lanes], rows)
+                rows = jnp.where(rep == r, ids_ref[slot : slot + 1, at], rows)
             rows = rows + shift
             here = (rows >= 0) & (rows < owned)
             rows = rows - first * step
@@ -94,9 +99,9 @@
 
         lax.fori_loop(bounds[j], bounds[j + 1], chunk, 0)
 
-        def some_blocks(i, carry, j=j):
+        def some_blocks(i, carry, j=j, out_ref=None, ahead=0):
             def some(n, carry):
-                at = j * blocks + i * batch + n
+                at = j * blocks + ahead + i * batch + n
                 to = n * lanes
                 for u in range(lanes):
                     stage[pl.ds(to + u, 1), :] = tab[pl.ds(row_ref[at, u], 1), :]
@@ -106,18 +111,22 @@
             for g in range(batch):
                 b = i * batch + g
                 turned = stage[g * lanes : (g + 1) * lanes].astype(BF16).T.astype(F32)
-                odd = odd_ref[pl.ds(j * blocks + b, 1), :] > 0
+                odd = odd_ref[pl.ds(j * blocks + ahead + b, 1), :] > 0
                 out_ref[b, j] = jnp.where(odd, turned[width:], turned[:width]).astype(BF16)
             return carry
 
-        lax.fori_loop(0, blocks // batch, some_blocks, 0)
-
-
-def lookup(ids, table_t, blocks, slot_of, shift_of, bounds_of, step, most):
+        for n, out_ref in enumerate(outs):
+            here = functools.partial(some_blocks, out_ref=out_ref, ahead=n * chips)
+            lax.fori_loop(0, chips // batch, here, 0)
+
+
+def lookup(ids, table_t, chips, slot_of, shift_of, bounds_of, step, most):
     width, owned = table_t.shape
     slots = len(slot_of)
     buffers = min(4, owned // step)
-    batch = divisor(blocks, (4, 2, 1))
+    reps = len(bounds_of[0])
+    blocks = chips * reps
+    batch = divisor(chips, (4, 2, 1))
     vmem = pl.BlockSpec(memory_space=pltpu.VMEM)
     anywhere = pl.BlockSpec(memory_space=pl.ANY)
     return pl.pallas_call(
@@ -129,9 +138,9 @@
             bounds_of=bounds_of,
             owned=owned,
         ),
-        out_shape=jax.ShapeDtypeStruct((blocks, slots, width, LANES), BF16),
+        out_shape=[jax.ShapeDtypeStruct((chips, slots, width, LANES), BF16)] * reps,
         in_specs=[vmem, anywhere],
-        out_specs=vmem,
+        out_specs=[vmem] * reps,
         scratch_shapes=[
             pltpu.VMEM((buffers, width, step), BF16),
             pltpu.VMEM((most // 2 + 8, 2 * width), F32),
@@ -149,6 +158,72 @@
     )(ids, table_t)
 
 
+def pack_kernel(*refs, sources, reps, chips):
+    found, outs = refs[:reps], refs[reps:]
+    rep = lax.axis_index("rep")
+    chip = lax.axis_index("fld")
+    for k in range(chips):
+        for s, parts in enumerate(sources):
+            total = None
+            for r, j in parts:
+                piece = found[0][k, j]
+                for n in range(1, reps):
+                    piece = jnp.where(lax.rem(rep + reps - n, reps) == r, found[n][k, j], piece)
+                total = piece if total is None else total + piece
+            if len(outs) == chips:
+                outs[k][s] = total
+            else:
+                outs[0][lax.rem(chip + k, chips), s] = total
+
+
+def pack(found, sources, single):
+    reps = len(found)
+    chips, _, width, lanes = found[0].shape
+    per = len(sources)
+    vmem = pl.BlockSpec(memory_space=pltpu.VMEM)
+    block = jax.ShapeDtypeStruct((per, width, lanes), BF16)
+    outs = [jax.ShapeDtypeStruct((chips, *block.shape), BF16)] if single else [block] * chips
+    return pl.pallas_call(
+        functools.partial(pack_kernel, sources=sources, reps=reps, chips=chips),
+        out_shape=outs,
+        in_specs=[vmem] * reps,
+        out_specs=[vmem] * len(outs),
+        compiler_params=pltpu.CompilerParams(vmem_limit_bytes=VMEM_BYTES),
+        name="pack",
+    )(*found)
+
+
+def join_kernel(*refs):
+    parts, out_ref = refs[:-1], refs[-1]
+    chips = len(parts)
+    lanes = parts[0].shape[-1]
+    chip = lax.axis_index("fld")
+    for k, part in enumerate(parts):
+        at = pl.multiple_of(lax.rem(chip + chips - k, chips) * lanes, lanes)
+        out_ref[:, :, pl.ds(at, lanes)] = part[...]
+
+
+def join(parts):
+    per, width, lanes = parts[0].shape
+    vmem = pl.BlockSpec(memory_space=pltpu.VMEM)
+    return pl.pallas_call(
+        join_kernel,
+        out_shape=jax.ShapeDtypeStruct((per, width, lanes * len(parts)), BF16),
+        in_specs=[vmem] * len(parts),
+        out_specs=vmem,
+        compiler_params=pltpu.CompilerParams(vmem_limit_bytes=VMEM_BYTES),
+        name="join",
+    )(*parts)
+
+
+def swap(blocks):
+    chips = len(blocks)
+    out = [blocks[0]]
+    for k in range(1, chips):
+        out.append(lax.ppermute(blocks[k], "fld", [(i, (i + k) % chips) for i in range(chips)]))
+    return out
+
+
 ROWS = 8
 CHAINS = 4
 
@@ -208,7 +283,7 @@
     jobs += [left[n : n + CHAINS] for n in range(0, len(left), CHAINS)]
 
     def some(i, carry):
-        own = [field_of(i * group + u) for u in range(group)]
+        own = [field_of(i, u) for u in range(group)]
         for h in range(HEADS):
             scores = {}
             for job in jobs:
@@ -239,7 +314,7 @@
                         sums[t] = sums[t] + term if t in sums else term
                 mixed = jnp.concatenate([halves(x) for x in sums.values()], axis=0)
                 out = mixed + r_s[own[u], h * size : (h + 1) * size, :]
-                store(i * group + u, h * size, jnp.maximum(out, 0.0).astype(BF16))
+                store(i, u, h * size, jnp.maximum(out, 0.0).astype(BF16))
         return carry
 
     lax.fori_loop(0, count // group, some, 0)
@@ -249,37 +324,26 @@
     return jnp.concatenate([ref[l].astype(F32).T.astype(BF16) for ref in refs], axis=0)
 
 
-def interact_kernel(place_ref, wq_ref, wk_ref, wv_ref, wr_ref, *refs, cuts, sources, group, part, opens):
-    count = len(cuts) if opens else 1
-    in_refs, o_ref = refs[:count], refs[count]
-    refs = refs[count + 1 :]
-    q_s, kt_s, k_s, v_s, r_s, a_s = refs[-6:]
-    chips, out_slots, width, lanes = o_ref.shape
-    fields = q_s.shape[0]
+def interact_kernel(place_ref, wq_ref, wk_ref, wv_ref, wr_ref, *refs, chips, group, fields):
+    q_s, kt_s, k_s, v_s, r_s, a_s, x_s, h_s = refs[-8:]
+    blocks = (len(refs) - 8) // 2
+    ins, outs = refs[:blocks], refs[blocks : 2 * blocks]
+    per, width, lanes = ins[0].shape[-3:]
     layers = wq_ref.shape[0]
     size = width // HEADS
-    per = len(sources)
     whole = chips * per == fields
+    chip = lax.axis_index("fld")
     weights = (wq_ref, wk_ref, wv_ref, wr_ref)
 
-    if opens:
-        x_s, h_s = refs[-7], refs[0]
-
-        def gather(i, carry):
-            for local, parts in enumerate(sources):
-                found = None
-                for r, j in parts:
-                    cut = next(n for n, (low, high) in enumerate(cuts) if low <= j < high)
-                    piece = in_refs[cut][i, r, j - cuts[cut][0]]
-                    found = piece if found is None else found + piece
-                x_s[i * per + local] = found
-            return carry
-
-        lax.fori_loop(0, chips, gather, 0)
-    else:
-        h_s = in_refs[0]
-
-    for l in range(0 if opens else layers - 1, layers):
+    def in_order(i, u):
+        return i * group + u
+
+    for k in range(chips):
+        back = lax.rem(chip + chips - k, chips)
+        for s in range(per):
+            x_s[back * per + s] = ins[k][s] if blocks == chips else ins[0][back, s]
+
+    for l in range(layers):
         if l == 0:
             load = lambda f: x_s[f if whole else place_ref[f]]
         else:
@@ -287,43 +351,38 @@
         project(load, layer_weights(weights, l), q_s, kt_s, k_s, v_s, r_s)
         if l < layers - 1:
 
-            def store(f, at, out):
-                h_s[f, at : at + size, :] = out
-
-            attend(q_s, k_s, v_s, r_s, a_s, store, lambda f: f, fields, group)
-        elif whole:
-
-            def store(n, at, out):
-                o_ref[lax.rem(n, chips), lax.div(n, chips), at : at + size, :] = out
-
-            def field_of(n):
-                return lax.rem(n, chips) * per + lax.div(n, chips) + part[0]
-
-            total = chips * out_slots
-            attend(q_s, k_s, v_s, r_s, a_s, store, field_of, total, group)
+            def store(i, u, at, out):
+                h_s[i * group + u, at : at + size, :] = out
+
+            attend(q_s, k_s, v_s, r_s, a_s, store, in_order, fields, group)
+        elif blocks == chips:
+            for low in range(0, chips, group):
+
+                def field_of(i, u, low=low):
+                    return lax.rem(chip + low + u, chips) * per + i
+
+                def store(i, u, at, out, low=low):
+                    outs[low + u][i, at : at + size, :] = out
+
+                attend(q_s, k_s, v_s, r_s, a_s, store, field_of, per * group, group)
         else:
-
-            def clear(i, carry):
-                for local in range(out_slots):
-                    o_ref[i, local] = jnp.zeros((width, lanes), BF16)
-                return carry
-
-            lax.fori_loop(0, chips, clear, 0)
-
-            def store(f, at, out):
-                slot = place_ref[f]
-                o_ref[lax.div(slot, per), lax.rem(slot, per), at : at + size, :] = out
-
-            attend(q_s, k_s, v_s, r_s, a_s, store, lambda f: f, fields, group)
-
-
-def interact(place, given, chips, cuts, weights, sources, fields, part, opens, more):
-    width, lanes = given[0].shape[-2:]
-    group = divisor(fields, (4, 2, 1))
+            for k in range(chips if not whole else 0):
+                for s in range(per):
+                    outs[0][k, s] = jnp.zeros((width, lanes), BF16)
+
+            def store(i, u, at, out):
+                f = i * group + u
+                slot = f if whole else place_ref[f]
+                outs[0][lax.div(slot, per), lax.rem(slot, per), at : at + size, :] = out
+
+            attend(q_s, k_s, v_s, r_s, a_s, store, in_order, fields, group)
+
+
+def interact(place, given, chips, weights, fields):
+    per, width, lanes = given[0].shape[-3:]
+    group = divisor(math.gcd(fields, chips), (4, 2, 1))
     wide = pltpu.VMEM((fields, width, lanes), F32)
     vmem = pl.BlockSpec(memory_space=pltpu.VMEM)
-    layer_in = jax.ShapeDtypeStruct((fields, width, lanes), BF16)
-    outs = [jax.ShapeDtypeStruct((chips, part[1] - part[0], width, lanes), BF16)]
     scratch = [
         wide,
         pltpu.VMEM((width * fields, lanes), F32),
@@ -331,26 +390,55 @@
         pltpu.VMEM((fields // 2, 2 * width, lanes), BF16),
         wide,
         pltpu.VMEM((group * fields, lanes), F32),
+        pltpu.VMEM((chips * per, width, lanes), BF16),
+        pltpu.VMEM((fields, width, lanes), BF16),
     ]
-    if opens:
-        scratch = [pltpu.VMEM((chips * len(sources), width, lanes), BF16)] + scratch
-        if more:
-            outs.append(layer_in)
-        else:
-            scratch = [pltpu.VMEM((fields, width, lanes), BF16)] + scratch
     return pl.pallas_call(
-        functools.partial(
-            interact_kernel, cuts=tuple(cuts), sources=sources, group=group, part=part, opens=opens
-        ),
-        out_shape=outs,
+        functools.partial(interact_kernel, chips=chips, group=group, fields=fields),
+        out_shape=[jax.ShapeDtypeStruct(x.shape, BF16) for x in given],
         in_specs=[pl.BlockSpec(memory_space=pltpu.SMEM)] + [vmem] * (4 + len(given)),
-        out_specs=[vmem] * len(outs),
+        out_specs=[vmem] * len(given),
         scratch_shapes=scratch,
         compiler_params=pltpu.CompilerParams(vmem_limit_bytes=VMEM_BYTES),
         cost_estimate=pl.CostEstimate(
             flops=12_000_000_000, bytes_accessed=4_000_000, transcendentals=0
         ),
+        name="interact",
     )(place, *weights, *given)
+
+
+def logit_kernel(w_ref, *refs):
+    blocks, o_ref = refs[:-1], refs[-1]
+    per, width, lanes = blocks[0].shape
+    total = jnp.zeros((ROWS, lanes), F32)
+    for k, block in enumerate(blocks):
+        rest = w_ref[k : k + 1, :]
+        pieces = []
+        for _ in range(3):
+            piece = rest.astype(BF16)
+            rest = rest - piece.astype(F32)
+            pieces.append(piece.astype(F32))
+        pieces.append(jnp.zeros((ROWS - 3, per * width), F32))
+        left = jnp.concatenate(pieces, axis=0).astype(BF16)
+        right = block[...].reshape(per * width, lanes)
+        total = total + jnp.dot(left, right, preferred_element_type=F32)
+    o_ref[...] = jnp.sum(total, axis=0, keepdims=True)
+
+
+def logit(weight, blocks):
+    lanes = blocks[0].shape[-1]
+    vmem = pl.BlockSpec(memory_space=pltpu.VMEM)
+    return pl.pallas_call(
+        logit_kernel,
+        out_shape=jax.ShapeDtypeStruct((1, lanes), F32),
+        in_specs=[vmem] * (1 + len(blocks)),
+        out_specs=vmem,
+        compiler_params=pltpu.CompilerParams(vmem_limit_bytes=VMEM_BYTES),
+        cost_estimate=pl.CostEstimate(
+            flops=1_000_000_000, bytes_accessed=1_000_000, transcendentals=0
+        ),
+        name="logit",
+    )(weight, *blocks)
 
 
 def per_device(
@@ -369,7 +457,6 @@
     reps = lax.axis_size("rep")
     half = total // reps
     peer = half // chips
-    blocks = chips * reps
     rows_slot = owned * reps // per
     slot_count = chips * per
     fields = field_slot.shape[0]
@@ -397,53 +484,41 @@
         ]
         most = max(end - start for end, start in zip(bounds_of[-1], starts)) * step
         slot_of = [[held_slots[r][j] for r in ranks] for j in range(low, high)]
-        return lookup(slot_ids, table_t, blocks, slot_of, shift_of, bounds_of, step, most)
-
-    def exchange(found):
-        arrived = lax.all_to_all(found, ("fld", "rep"), 0, 0, tiled=True)
-        return arrived.reshape(chips, reps, found.shape[1], width, peer)
-
-    cuts = [(0, held)]
-    founds = []
-    for cut in cuts:
-        founds.append(look_up(*cut))
-    arrived = []
-    for found in founds:
-        arrived.append(exchange(found))
+        return lookup(slot_ids, table_t, chips, slot_of, shift_of, bounds_of, step, most)
+
+    found = look_up(0, held)
+    found = [found[0]] + [
+        lax.ppermute(found[n], "rep", [(r, (r + n) % reps) for r in ranks]) for n in range(1, reps)
+    ]
+    single = slot_count != fields or chips > 8
+    blocks = pack(found, sources, single)
+
+    def exchange(blocks):
+        if single:
+            return [lax.all_to_all(blocks[0], "fld", 0, 0, tiled=True)]
+        return swap(blocks)
+
     weights = (query_weight, key_weight, value_weight, residual_weight)
-
-    parts = parts_of(per)
-    given = arrived
-    hidden, sent = [], []
-    for n, part in enumerate(parts):
-        more = n + 1 < len(parts)
-        done = interact(
-            field_slot, given, chips, cuts, weights, sources, fields, part, n == 0, more
-        )
-        hidden.append(done[0])
-        given = done[1:] if n == 0 else given
-    for block in hidden:
-        sent.append(lax.all_to_all(block, "fld", 0, 0, tiled=True))
-    select = (field_slot[:, None] == jnp.arange(slot_count, dtype=jnp.int32)[None, :]).astype(F32)
+    hidden = interact(field_slot, exchange(blocks), chips, weights, fields)
+    sent = exchange(hidden)
+
+    slots = jnp.arange(slot_count, dtype=jnp.int32)
+    if not single:
+        slots = (slots + lax.axis_index("fld") * per) % slot_count
+    select = (field_slot[:, None] == slots[None, :]).astype(F32)
     slot_weight = jnp.einsum("fs,fd->sd", select, out_weight, precision=lax.Precision.HIGHEST)
-    slot_weight = slot_weight.reshape(chips, per, width)
-    logits = sum(
-        jnp.einsum(
+    if single:
+        logits = jnp.einsum(
             "csdn,csd->n",
-            block.astype(F32),
-            slot_weight[:, low:high],
+            hidden[0].astype(F32),
+            slot_weight.reshape(chips, per, width),
             precision=lax.Precision.HIGHEST,
-        )
-        for block, (low, high) in zip(hidden, parts)
-    )
-    interacted = jnp.concatenate(
-        [x.transpose(1, 0, 3, 2).reshape(x.shape[1], half, width) for x in sent], axis=0
-    )
-    return (interacted, logits.reshape(1, peer))
-
-
-def parts_of(per):
-    return [(0, per)]
+        ).reshape(1, peer)
+        joined = sent[0].transpose(1, 2, 0, 3).reshape(per, width, half)
+    else:
+        logits = logit(slot_weight.reshape(chips, per * width), hidden)
+        joined = join(sent)
+    return (jnp.transpose(joined, (0, 2, 1)), logits)
 
 
 def solution(mesh):

time: 80.6 us -> 79.2 us (0.983)
  blocking collectives: 27.6 us -> 0 us
  starting transfers between devices: 3.83 us -> 28.5 us
  Pallas kernels: 28.8 us -> 34.3 us
  waiting for transfers between devices: 16 us -> 12.2 us
  matrix products: 2.31 us -> 0.28 us
  local copies, waits for them, and re-layouts: 0.95 us -> 2.73 us
    ppermute x0 -> x15, starting transfers between devices: none -> 28.5 us  [the longest x14 28 us: swap(): lax.ppermute(blocks[k], 'fld', [(i, (i + k) % chips) for i in range(chips)])]
    all_to_all x1 -> x0, blocking collectives: 27.6 us -> none  [exchange(): arrived = lax.all_to_all(found, ('fld', 'rep'), 0, 0, tiled=True)]
    all_to_all x1 -> x0, waiting for transfers between devices: 16 us -> none  [per_device(): sent.append(lax.all_to_all(block, 'fld', 0, 0, tiled=True))]
    ppermute x0 -> x15, waiting for transfers between devices: none -> 12.2 us  [the longest x14 10.7 us: swap(): lax.ppermute(blocks[k], 'fld', [(i, (i + k) % chips) for i in range(chips)])]
    pallas_call x1 -> x4, Pallas kernels: 13.2 us -> 18.8 us  [the longest x1 12.6 us: interact(): pl.pallas_call(functools.partial(interact_kernel, chips=chips, group=grou...]
    all_to_all x1 -> x0, starting transfers between devices: 3.83 us -> none  [per_device(): sent.append(lax.all_to_all(block, 'fld', 0, 0, tiled=True))]
    unnamed x4 -> x34, local copies, waits for them, and re-layouts: 0.01 us -> 2.05 us
    dot_general x1 -> x0, matrix products: 2.03 us -> none  [per_device(): jnp.einsum('csdn,csd->n', block.astype(F32), slot_weight[:, low:high], pr...]
  transfers between devices with their start and end apart: 1 -> 15, of which waited for: 1 -> 7; matrix products, arithmetic and copies ran while one was open for 3% -> 1% of each run, Pallas kernels for 0% -> 2%
where the time goes in v2:
time: 79.2 us; the launch traced here: 78.8 us
  Pallas kernels  34.3 us (43%)
  starting transfers between devices  28.5 us (36%)
  waiting for transfers between devices  12.2 us (15%)
  local copies, waits for them, and re-layouts  2.73 us (3%)
    ppermute x14, starting transfers between devices, swap(): lax.ppermute(blocks[k], 'fld', [(i, (i + k) % chips) for i in range(chips)])  28 us
    pallas_call x1, Pallas kernels, lookup(): pl.pallas_call(functools.partial(lookup_kernel, step=step, slot_of=slot_o...  15.5 us
    pallas_call x1, Pallas kernels, interact(): pl.pallas_call(functools.partial(interact_kernel, chips=chips, group=grou...  12.6 us
    ppermute x14, waiting for transfers between devices, swap(): lax.ppermute(blocks[k], 'fld', [(i, (i + k) % chips) for i in range(chips)])  10.7 us
    pallas_call x1, Pallas kernels, join(): pl.pallas_call(join_kernel, out_shape=jax.ShapeDtypeStruct((per, width, l...  2.2 us
    pallas_call x1, Pallas kernels, pack(): pl.pallas_call(functools.partial(pack_kernel, sources=sources, reps=reps,...  2.08 us
    unnamed x34, local copies, waits for them, and re-layouts  2.05 us
    pallas_call x1, Pallas kernels, logit(): pl.pallas_call(logit_kernel, out_shape=jax.ShapeDtypeStruct((1, lanes), F...  1.93 us
  transfers between devices with their start and end apart: 15, of which 7 were waited for; matrix products, arithmetic and copies ran while one was open for 1% of the time, Pallas kernels for 2%

profile of v2, /device:TPU:0, one launch (start us, length us, event | category | flops | bytes accessed | tf_op | source)
XLA Modules:
  0.0 78.8 jit_solution(8275135135063086713)
XLA Ops:
  0.6 15.5 %shard_map.95 = (bf16[8,3,64,128]{3,2,1,0:T(8,128)(2,1)}, bf16[8,3,64,128]{3,2,1,0:T(8,128)(2,1)}) custom-call(s32[5,2048]{1,0:T(8,128)} %bitcast.6, bf16[64,163840]{1,0:T(8,128)(2,1)} %bitcast.5), custom_call_target="tpu_custom_call" | custom-call | flops 35999997952 | bytes 20971520 | tf_op jit(solution)/shard_map/pallas_call | solution.py:132
  16.1 0.5 collective-permute-start
  16.6 1.6 %collective-permute-done.refs_1_ = bf16[8,3,64,128]{3,2,1,0:T(8,128)(2,1)S(1)} collective-permute-done((bf16[8,3,64,128]{3,2,1,0:T(8,128)(2,1)}, bf16[8,3,64,128]{3,2,1,0:T(8,128)(2,1)S(1)}, u32[]{:S(2)}, u32[]{:S(2)}) %collective-permute-start) | collective-permute-done | bytes 393248 | tf_op jit(solution)/shard_map/ppermute | solution.py:491
  18.2 0.8 copy-done.1
  18.9 2.1 %pack.1 = (bf16[5,64,128]{2,1,0:T(8,128)(2,1)}, bf16[5,64,128]{2,1,0:T(8,128)(2,1)}, bf16[5,64,128]{2,1,0:T(8,128)(2,1)}, bf16[5,64,128]{2,1,0:T(8,128)(2,1)}, b...) custom-call(bf16[8,3,64,128]{3,2,1,0:T(8,128)(2,1)} %get-tuple-eleme, ...), custom_call_target="tpu_custom_call" | custom-call | tf_op jit(solution)/shard_map/pack/pallas_call | solution.py:186
  21.0 2.9 %collective-permute-start.1 = (bf16[5,64,128]{2,1,0:T(8,128)(2,1)}, bf16[5,64,128]{2,1,0:T(8,128)(2,1)S(1)}, u32[]{:S(2)}, u32[]{:S(2)}) collective-permute-start(bf16[5,64,128]{2,1,0:T(8,128)(2,1)} %get-tuple-element.23), channel_id=1, source_target_pairs={{0,2},{2,4},{4,6},{6,8},{8,10},{10,12},{12,14},{14,0},{1,3},{3,5},... | collective-permute-start | bytes 245768 | tf_op jit(solution)/shard_map/ppermute | solution.py:223
  23.9 1.6 %collective-permute-start.2 = (bf16[5,64,128]{2,1,0:T(8,128)(2,1)}, bf16[5,64,128]{2,1,0:T(8,128)(2,1)S(1)}, u32[]{:S(2)}, u32[]{:S(2)}) collective-permute-start(bf16[5,64,128]{2,1,0:T(8,128)(2,1)} %get-tuple-element.24), channel_id=1, source_target_pairs={{0,4},{2,6},{4,8},{6,10},{8,12},{10,14},{12,0},{14,2},{1,5},{3,7},... | collective-permute-start | bytes 245768 | tf_op jit(solution)/shard_map/ppermute | solution.py:223
  25.5 2.6 %collective-permute-start.3 = (bf16[5,64,128]{2,1,0:T(8,128)(2,1)}, bf16[5,64,128]{2,1,0:T(8,128)(2,1)S(1)}, u32[]{:S(2)}, u32[]{:S(2)}) collective-permute-start(bf16[5,64,128]{2,1,0:T(8,128)(2,1)} %get-tuple-element.25), channel_id=1, source_target_pairs={{0,6},{2,8},{4,10},{6,12},{8,14},{10,0},{12,2},{14,4},{1,7},{3,9},... | collective-permute-start | bytes 245768 | tf_op jit(solution)/shard_map/ppermute | solution.py:223
  28.1 1.2 %collective-permute-start.4 = (bf16[5,64,128]{2,1,0:T(8,128)(2,1)}, bf16[5,64,128]{2,1,0:T(8,128)(2,1)S(1)}, u32[]{:S(2)}, u32[]{:S(2)}) collective-permute-start(bf16[5,64,128]{2,1,0:T(8,128)(2,1)} %get-tuple-element.26), channel_id=1, source_target_pairs={{0,8},{2,10},{4,12},{6,14},{8,0},{10,2},{12,4},{14,6},{1,9},{3,11}... | collective-permute-start | bytes 245768 | tf_op jit(solution)/shard_map/ppermute | solution.py:223
  29.3 2.6 %collective-permute-start.5 = (bf16[5,64,128]{2,1,0:T(8,128)(2,1)}, bf16[5,64,128]{2,1,0:T(8,128)(2,1)S(1)}, u32[]{:S(2)}, u32[]{:S(2)}) collective-permute-start(bf16[5,64,128]{2,1,0:T(8,128)(2,1)} %get-tuple-element.27), channel_id=1, source_target_pairs={{0,10},{2,12},{4,14},{6,0},{8,2},{10,4},{12,6},{14,8},{1,11},{3,13... | collective-permute-start | bytes 245768 | tf_op jit(solution)/shard_map/ppermute | solution.py:223
  31.9 1.3 %collective-permute-start.6 = (bf16[5,64,128]{2,1,0:T(8,128)(2,1)}, bf16[5,64,128]{2,1,0:T(8,128)(2,1)S(1)}, u32[]{:S(2)}, u32[]{:S(2)}) collective-permute-start(bf16[5,64,128]{2,1,0:T(8,128)(2,1)} %get-tuple-element.28), channel_id=1, source_target_pairs={{0,12},{2,14},{4,0},{6,2},{8,4},{10,6},{12,8},{14,10},{1,13},{3,15... | collective-permute-start | bytes 245768 | tf_op jit(solution)/shard_map/ppermute | solution.py:223
  33.3 1.4 %collective-permute-start.7 = (bf16[5,64,128]{2,1,0:T(8,128)(2,1)}, bf16[5,64,128]{2,1,0:T(8,128)(2,1)S(1)}, u32[]{:S(2)}, u32[]{:S(2)}) collective-permute-start(bf16[5,64,128]{2,1,0:T(8,128)(2,1)} %get-tuple-element.29), channel_id=1, source_target_pairs={{0,14},{2,0},{4,2},{6,4},{8,6},{10,8},{12,10},{14,12},{1,15},{3,1}... | collective-permute-start | bytes 245768 | tf_op jit(solution)/shard_map/ppermute | solution.py:223
  34.7 2.4 %collective-permute-done.3.refs_3_ = bf16[5,64,128]{2,1,0:T(8,128)(2,1)S(1)} collective-permute-done((bf16[5,64,128]{2,1,0:T(8,128)(2,1)}, bf16[5,64,128]{2,1,0:T(8,128)(2,1)S(1)}, u32[]{:S(2)}, u32[]{:S(2)}) %collective-permute-start.3) | collective-permute-done | bytes 81952 | tf_op jit(solution)/shard_map/ppermute | solution.py:223
  37.1 0.7 collective-permute-done.4.refs_4_
  37.9 1.9 %collective-permute-done.6.refs_6_ = bf16[5,64,128]{2,1,0:T(8,128)(2,1)S(1)} collective-permute-done((bf16[5,64,128]{2,1,0:T(8,128)(2,1)}, bf16[5,64,128]{2,1,0:T(8,128)(2,1)S(1)}, u32[]{:S(2)}, u32[]{:S(2)}) %collective-permute-start.6) | collective-permute-done | bytes 81952 | tf_op jit(solution)/shard_map/ppermute | solution.py:223
  39.8 0.6 copy-done.14
  40.4 0.0 copy-done.15
  40.5 12.6 %interact.1 = (bf16[5,64,128]{2,1,0:T(8,128)(2,1)}, bf16[5,64,128]{2,1,0:T(8,128)(2,1)}, bf16[5,64,128]{2,1,0:T(8,128)(2,1)}, bf16[5,64,128]{2,1,0:T(8,128)(2,1)...) custom-call(s32[40]{0:T(128)} %place_ref.1, ...), custom_call_target="tpu_custom_call" | custom-call | flops 12000000000 | bytes 4000000 | tf_op jit(solution)/shard_map/interact/pallas_call | solution.py:396
  53.1 4.6 %collective-permute-start.10 = (bf16[5,64,128]{2,1,0:T(8,128)(2,1)}, bf16[5,64,128]{2,1,0:T(8,128)(2,1)S(1)}, u32[]{:S(2)}, u32[]{:S(2)}) collective-permute-start(bf16[5,64,128]{2,1,0:T(8,128)(2,1)} %get-tuple-element.33.refs_3_), channel_id=1, source_target_pairs={{0,6},{2,8},{4,10},{6,12},{8,14},{10,0},{12,2},{14,4},{1,7},{3,9},... | collective-permute-start | bytes 245768 | tf_op jit(solution)/shard_map/ppermute | solution.py:223
  57.7 1.4 %collective-permute-start.11 = (bf16[5,64,128]{2,1,0:T(8,128)(2,1)}, bf16[5,64,128]{2,1,0:T(8,128)(2,1)S(1)}, u32[]{:S(2)}, u32[]{:S(2)}) collective-permute-start(bf16[5,64,128]{2,1,0:T(8,128)(2,1)} %get-tuple-element.34.refs_4_), channel_id=1, source_target_pairs={{0,8},{2,10},{4,12},{6,14},{8,0},{10,2},{12,4},{14,6},{1,9},{3,11}... | collective-permute-start | bytes 245768 | tf_op jit(solution)/shard_map/ppermute | solution.py:223
  59.0 0.3 fusion
  59.3 0.7 reshape.18.w_ref
  60.0 1.3 %collective-permute-start.12 = (bf16[5,64,128]{2,1,0:T(8,128)(2,1)}, bf16[5,64,128]{2,1,0:T(8,128)(2,1)S(1)}, u32[]{:S(2)}, u32[]{:S(2)}) collective-permute-start(bf16[5,64,128]{2,1,0:T(8,128)(2,1)} %get-tuple-element.35.refs_5_), channel_id=1, source_target_pairs={{0,10},{2,12},{4,14},{6,0},{8,2},{10,4},{12,6},{14,8},{1,11},{3,13... | collective-permute-start | bytes 245768 | tf_op jit(solution)/shard_map/ppermute | solution.py:223
  61.3 1.5 %collective-permute-start.13 = (bf16[5,64,128]{2,1,0:T(8,128)(2,1)}, bf16[5,64,128]{2,1,0:T(8,128)(2,1)S(1)}, u32[]{:S(2)}, u32[]{:S(2)}) collective-permute-start(bf16[5,64,128]{2,1,0:T(8,128)(2,1)} %get-tuple-element.36.refs_6_), channel_id=1, source_target_pairs={{0,12},{2,14},{4,0},{6,2},{8,4},{10,6},{12,8},{14,10},{1,13},{3,15... | collective-permute-start | bytes 245768 | tf_op jit(solution)/shard_map/ppermute | solution.py:223
  62.7 1.5 %collective-permute-start.14 = (bf16[5,64,128]{2,1,0:T(8,128)(2,1)}, bf16[5,64,128]{2,1,0:T(8,128)(2,1)S(1)}, u32[]{:S(2)}, u32[]{:S(2)}) collective-permute-start(bf16[5,64,128]{2,1,0:T(8,128)(2,1)} %get-tuple-element.37.refs_7_), channel_id=1, source_target_pairs={{0,14},{2,0},{4,2},{6,4},{8,6},{10,8},{12,10},{14,12},{1,15},{3,1}... | collective-permute-start | bytes 245768 | tf_op jit(solution)/shard_map/ppermute | solution.py:223
  64.2 0.6 collective-permute-done.10.refs_3_
  64.8 1.6 %collective-permute-done.11.refs_4_ = bf16[5,64,128]{2,1,0:T(8,128)(2,1)S(1)} collective-permute-done((bf16[5,64,128]{2,1,0:T(8,128)(2,1)}, bf16[5,64,128]{2,1,0:T(8,128)(2,1)S(1)}, u32[]{:S(2)}, u32[]{:S(2)}) %collective-permute-start.11) | collective-permute-done | bytes 81952 | tf_op jit(solution)/shard_map/ppermute | solution.py:223
  66.5 4.2 %collective-permute-start.9 = (bf16[5,64,128]{2,1,0:T(8,128)(2,1)}, bf16[5,64,128]{2,1,0:T(8,128)(2,1)S(1)}, u32[]{:S(2)}, u32[]{:S(2)}) collective-permute-start(bf16[5,64,128]{2,1,0:T(8,128)(2,1)} %get-tuple-element.32.refs_2_), channel_id=1, source_target_pairs={{0,4},{2,6},{4,8},{6,10},{8,12},{10,14},{12,0},{14,2},{1,5},{3,7},... | collective-permute-start | bytes 245768 | tf_op jit(solution)/shard_map/ppermute | solution.py:223
  70.6 1.9 %logit.1 = f32[1,128]{1,0:T(1,128)} custom-call(f32[8,320]{1,0:T(8,128)} %reshape.18.w_ref, bf16[5,64,128]{2,1,0:T(8,128)(2,1)} %get-tuple-element.30.refs_0_, bf16[5,64,128]{2,1,0:T(8,128)(2,1)} %get-tuple-element.31.refs_1_, bf16[5,64,128]{2,1,0:T(8,128)(2,1)} %get-tuple-element.32.refs_2_, bf16[5,64,128]{2,1,0:T(8,128)(2,1)} %get-tuple-element.33.refs_3_, ...), custom_call_target="tpu_custom_call" | custom-call | flops 1000000000 | bytes 1000000 | tf_op jit(solution)/shard_map/logit/pallas_call | solution.py:431
  72.6 3.3 %collective-permute-done.9.refs_2_ = bf16[5,64,128]{2,1,0:T(8,128)(2,1)S(1)} collective-permute-done((bf16[5,64,128]{2,1,0:T(8,128)(2,1)}, bf16[5,64,128]{2,1,0:T(8,128)(2,1)S(1)}, u32[]{:S(2)}, u32[]{:S(2)}) %collective-permute-start.9) | collective-permute-done | bytes 81952 | tf_op jit(solution)/shard_map/ppermute | solution.py:223
  76.0 0.6 copy-done.8
  76.6 2.2 %join.1 = bf16[5,64,1024]{2,1,0:T(8,128)(2,1)} custom-call(bf16[5,64,128]{2,1,0:T(8,128)(2,1)} %get-tuple-element.30.refs_0_, bf16[5,64,128]{2,1,0:T(8,128)(2,1)} %copy-done.7, bf16[5,64,128]{2,1,0:T(8,128)(2,1)} %copy-done.8, bf16[5,64,128]{2,1,0:T(8,128)(2,1)} %copy-done.2, bf16[5,64,128]{2,1,0:T(8,128)(2,1)} %copy-done.3, bf16[5,64,128]{2,1,0:T(8,128)(2,1)} %copy-done.4, ...), custom_call_target="tpu_custom_call" | custom-call | tf_op jit(solution)/shard_map/join/pallas_call | solution.py:209
  (40 shorter events, 0.1 us)
Async XLA Ops:
  0.6 58.4 %copy-start = (f32[40,64]{1,0:T(8,128)S(1)}, f32[40,64]{1,0:T(8,128)}, u32[]{:S(2)}) copy-start(f32[40,64]{1,0:T(8,128)} %param.15) | copy-start | bytes 30724
  16.1 2.1 %collective-permute-start = (bf16[8,3,64,128]{3,2,1,0:T(8,128)(2,1)}, bf16[8,3,64,128]{3,2,1,0:T(8,128)(2,1)S(1)}, u32[]{:S(2)}, u32[]{:S(2)}) collective-permute-start(bf16[8,3,64,128]{3,2,1,0:T(8,128)(2,1)} %get-tuple-element.21), channel_id=1, source_target_pairs={{0,1},{1,0},{2,3},{3,2},{4,5},{5,4},{6,7},{7,6},{8,9},{9,8},{10,11... | collective-permute-start | bytes 1179656 | tf_op jit(solution)/shard_map/ppermute | solution.py:491
  18.2 0.8 copy-start.1
  21.0 10.9 %collective-permute-start.1 = (bf16[5,64,128]{2,1,0:T(8,128)(2,1)}, bf16[5,64,128]{2,1,0:T(8,128)(2,1)S(1)}, u32[]{:S(2)}, u32[]{:S(2)}) collective-permute-start(bf16[5,64,128]{2,1,0:T(8,128)(2,1)} %get-tuple-element.23), channel_id=1, source_target_pairs={{0,2},{2,4},{4,6},{6,8},{8,10},{10,12},{12,14},{14,0},{1,3},{3,5},... | collective-permute-start | bytes 245768 | tf_op jit(solution)/shard_map/ppermute | solution.py:223
  23.9 9.3 %collective-permute-start.2 = (bf16[5,64,128]{2,1,0:T(8,128)(2,1)}, bf16[5,64,128]{2,1,0:T(8,128)(2,1)S(1)}, u32[]{:S(2)}, u32[]{:S(2)}) collective-permute-start(bf16[5,64,128]{2,1,0:T(8,128)(2,1)} %get-tuple-element.24), channel_id=1, source_target_pairs={{0,4},{2,6},{4,8},{6,10},{8,12},{10,14},{12,0},{14,2},{1,5},{3,7},... | collective-permute-start | bytes 245768 | tf_op jit(solution)/shard_map/ppermute | solution.py:223
  25.5 11.6 %collective-permute-start.3 = (bf16[5,64,128]{2,1,0:T(8,128)(2,1)}, bf16[5,64,128]{2,1,0:T(8,128)(2,1)S(1)}, u32[]{:S(2)}, u32[]{:S(2)}) collective-permute-start(bf16[5,64,128]{2,1,0:T(8,128)(2,1)} %get-tuple-element.25), channel_id=1, source_target_pairs={{0,6},{2,8},{4,10},{6,12},{8,14},{10,0},{12,2},{14,4},{1,7},{3,9},... | collective-permute-start | bytes 245768 | tf_op jit(solution)/shard_map/ppermute | solution.py:223
  28.1 9.8 %collective-permute-start.4 = (bf16[5,64,128]{2,1,0:T(8,128)(2,1)}, bf16[5,64,128]{2,1,0:T(8,128)(2,1)S(1)}, u32[]{:S(2)}, u32[]{:S(2)}) collective-permute-start(bf16[5,64,128]{2,1,0:T(8,128)(2,1)} %get-tuple-element.26), channel_id=1, source_target_pairs={{0,8},{2,10},{4,12},{6,14},{8,0},{10,2},{12,4},{14,6},{1,9},{3,11}... | collective-permute-start | bytes 245768 | tf_op jit(solution)/shard_map/ppermute | solution.py:223
  29.3 8.6 %collective-permute-start.5 = (bf16[5,64,128]{2,1,0:T(8,128)(2,1)}, bf16[5,64,128]{2,1,0:T(8,128)(2,1)S(1)}, u32[]{:S(2)}, u32[]{:S(2)}) collective-permute-start(bf16[5,64,128]{2,1,0:T(8,128)(2,1)} %get-tuple-element.27), channel_id=1, source_target_pairs={{0,10},{2,12},{4,14},{6,0},{8,2},{10,4},{12,6},{14,8},{1,11},{3,13... | collective-permute-start | bytes 245768 | tf_op jit(solution)/shard_map/ppermute | solution.py:223
  31.9 7.9 %copy-start.9 = (bf16[5,64,128]{2,1,0:T(8,128)(2,1)}, bf16[5,64,128]{2,1,0:T(8,128)(2,1)S(1)}, u32[]{:S(2)}) copy-start(bf16[5,64,128]{2,1,0:T(8,128)(2,1)S(1)} %collective-permute-done.1.refs_1_) | copy-start | bytes 245764
  31.9 7.9 %collective-permute-start.6 = (bf16[5,64,128]{2,1,0:T(8,128)(2,1)}, bf16[5,64,128]{2,1,0:T(8,128)(2,1)S(1)}, u32[]{:S(2)}, u32[]{:S(2)}) collective-permute-start(bf16[5,64,128]{2,1,0:T(8,128)(2,1)} %get-tuple-element.28), channel_id=1, source_target_pairs={{0,12},{2,14},{4,0},{6,2},{8,4},{10,6},{12,8},{14,10},{1,13},{3,15... | collective-permute-start | bytes 245768 | tf_op jit(solution)/shard_map/ppermute | solution.py:223
  33.3 6.5 %copy-start.10 = (bf16[5,64,128]{2,1,0:T(8,128)(2,1)}, bf16[5,64,128]{2,1,0:T(8,128)(2,1)S(1)}, u32[]{:S(2)}) copy-start(bf16[5,64,128]{2,1,0:T(8,128)(2,1)S(1)} %collective-permute-done.2.refs_2_) | copy-start | bytes 245764
  33.3 6.5 %collective-permute-start.7 = (bf16[5,64,128]{2,1,0:T(8,128)(2,1)}, bf16[5,64,128]{2,1,0:T(8,128)(2,1)S(1)}, u32[]{:S(2)}, u32[]{:S(2)}) collective-permute-start(bf16[5,64,128]{2,1,0:T(8,128)(2,1)} %get-tuple-element.29), channel_id=1, source_target_pairs={{0,14},{2,0},{4,2},{6,4},{8,6},{10,8},{12,10},{14,12},{1,15},{3,1}... | collective-permute-start | bytes 245768 | tf_op jit(solution)/shard_map/ppermute | solution.py:223
  37.1 2.7 %copy-start.11 = (bf16[5,64,128]{2,1,0:T(8,128)(2,1)}, bf16[5,64,128]{2,1,0:T(8,128)(2,1)S(1)}, u32[]{:S(2)}) copy-start(bf16[5,64,128]{2,1,0:T(8,128)(2,1)S(1)} %collective-permute-done.3.refs_3_) | copy-start | bytes 245764
  37.9 1.9 %copy-start.12 = (bf16[5,64,128]{2,1,0:T(8,128)(2,1)}, bf16[5,64,128]{2,1,0:T(8,128)(2,1)S(1)}, u32[]{:S(2)}) copy-start(bf16[5,64,128]{2,1,0:T(8,128)(2,1)S(1)} %collective-permute-done.4.refs_4_) | copy-start | bytes 245764
  37.9 1.9 %copy-start.13 = (bf16[5,64,128]{2,1,0:T(8,128)(2,1)}, bf16[5,64,128]{2,1,0:T(8,128)(2,1)S(1)}, u32[]{:S(2)}) copy-start(bf16[5,64,128]{2,1,0:T(8,128)(2,1)S(1)} %collective-permute-done.5.refs_5_) | copy-start | bytes 245764
  39.8 0.6 copy-start.14
  39.8 0.7 copy-start.15
  40.5 18.6 %copy-start.16 = (s32[40]{0:T(128)S(1)}, s32[40]{0:T(128)}, u32[]{:S(2)}) copy-start(s32[40]{0:T(128)} %place_ref.1) | copy-start | bytes 484
  53.1 11.8 %collective-permute-start.10 = (bf16[5,64,128]{2,1,0:T(8,128)(2,1)}, bf16[5,64,128]{2,1,0:T(8,128)(2,1)S(1)}, u32[]{:S(2)}, u32[]{:S(2)}) collective-permute-start(bf16[5,64,128]{2,1,0:T(8,128)(2,1)} %get-tuple-element.33.refs_3_), channel_id=1, source_target_pairs={{0,6},{2,8},{4,10},{6,12},{8,14},{10,0},{12,2},{14,4},{1,7},{3,9},... | collective-permute-start | bytes 245768 | tf_op jit(solution)/shard_map/ppermute | solution.py:223
  57.7 8.8 %collective-permute-start.11 = (bf16[5,64,128]{2,1,0:T(8,128)(2,1)}, bf16[5,64,128]{2,1,0:T(8,128)(2,1)S(1)}, u32[]{:S(2)}, u32[]{:S(2)}) collective-permute-start(bf16[5,64,128]{2,1,0:T(8,128)(2,1)} %get-tuple-element.34.refs_4_), channel_id=1, source_target_pairs={{0,8},{2,10},{4,12},{6,14},{8,0},{10,2},{12,4},{14,6},{1,9},{3,11}... | collective-permute-start | bytes 245768 | tf_op jit(solution)/shard_map/ppermute | solution.py:223
  60.0 12.6 %collective-permute-start.12 = (bf16[5,64,128]{2,1,0:T(8,128)(2,1)}, bf16[5,64,128]{2,1,0:T(8,128)(2,1)S(1)}, u32[]{:S(2)}, u32[]{:S(2)}) collective-permute-start(bf16[5,64,128]{2,1,0:T(8,128)(2,1)} %get-tuple-element.35.refs_5_), channel_id=1, source_target_pairs={{0,10},{2,12},{4,14},{6,0},{8,2},{10,4},{12,6},{14,8},{1,11},{3,13... | collective-permute-start | bytes 245768 | tf_op jit(solution)/shard_map/ppermute | solution.py:223
  61.3 11.3 %collective-permute-start.13 = (bf16[5,64,128]{2,1,0:T(8,128)(2,1)}, bf16[5,64,128]{2,1,0:T(8,128)(2,1)S(1)}, u32[]{:S(2)}, u32[]{:S(2)}) collective-permute-start(bf16[5,64,128]{2,1,0:T(8,128)(2,1)} %get-tuple-element.36.refs_6_), channel_id=1, source_target_pairs={{0,12},{2,14},{4,0},{6,2},{8,4},{10,6},{12,8},{14,10},{1,13},{3,15... | collective-permute-start | bytes 245768 | tf_op jit(solution)/shard_map/ppermute | solution.py:223
  62.7 9.9 %collective-permute-start.14 = (bf16[5,64,128]{2,1,0:T(8,128)(2,1)}, bf16[5,64,128]{2,1,0:T(8,128)(2,1)S(1)}, u32[]{:S(2)}, u32[]{:S(2)}) collective-permute-start(bf16[5,64,128]{2,1,0:T(8,128)(2,1)} %get-tuple-element.37.refs_7_), channel_id=1, source_target_pairs={{0,14},{2,0},{4,2},{6,4},{8,6},{10,8},{12,10},{14,12},{1,15},{3,1}... | collective-permute-start | bytes 245768 | tf_op jit(solution)/shard_map/ppermute | solution.py:223
  64.8 11.2 %copy-start.2 = (bf16[5,64,128]{2,1,0:T(8,128)(2,1)}, bf16[5,64,128]{2,1,0:T(8,128)(2,1)S(1)}, u32[]{:S(2)}) copy-start(bf16[5,64,128]{2,1,0:T(8,128)(2,1)S(1)} %collective-permute-done.10.refs_3_) | copy-start | bytes 245764
  64.8 7.8 %collective-permute-start.8 = (bf16[5,64,128]{2,1,0:T(8,128)(2,1)}, bf16[5,64,128]{2,1,0:T(8,128)(2,1)S(1)}, u32[]{:S(2)}, u32[]{:S(2)}) collective-permute-start(bf16[5,64,128]{2,1,0:T(8,128)(2,1)} %get-tuple-element.31.refs_1_), channel_id=1, source_target_pairs={{0,2},{2,4},{4,6},{6,8},{8,10},{10,12},{12,14},{14,0},{1,3},{3,5},... | collective-permute-start | bytes 245768 | tf_op jit(solution)/shard_map/ppermute | solution.py:223
  66.5 9.5 %copy-start.3 = (bf16[5,64,128]{2,1,0:T(8,128)(2,1)}, bf16[5,64,128]{2,1,0:T(8,128)(2,1)S(1)}, u32[]{:S(2)}) copy-start(bf16[5,64,128]{2,1,0:T(8,128)(2,1)S(1)} %collective-permute-done.11.refs_4_) | copy-start | bytes 245764
  66.5 9.5 %collective-permute-start.9 = (bf16[5,64,128]{2,1,0:T(8,128)(2,1)}, bf16[5,64,128]{2,1,0:T(8,128)(2,1)S(1)}, u32[]{:S(2)}, u32[]{:S(2)}) collective-permute-start(bf16[5,64,128]{2,1,0:T(8,128)(2,1)} %get-tuple-element.32.refs_2_), channel_id=1, source_target_pairs={{0,4},{2,6},{4,8},{6,10},{8,12},{10,14},{12,0},{14,2},{1,5},{3,7},... | collective-permute-start | bytes 245768 | tf_op jit(solution)/shard_map/ppermute | solution.py:223
  72.6 3.4 %copy-start.4 = (bf16[5,64,128]{2,1,0:T(8,128)(2,1)}, bf16[5,64,128]{2,1,0:T(8,128)(2,1)S(1)}, u32[]{:S(2)}) copy-start(bf16[5,64,128]{2,1,0:T(8,128)(2,1)S(1)} %collective-permute-done.12.refs_5_) | copy-start | bytes 245764
  72.6 3.4 %copy-start.5 = (bf16[5,64,128]{2,1,0:T(8,128)(2,1)}, bf16[5,64,128]{2,1,0:T(8,128)(2,1)S(1)}, u32[]{:S(2)}) copy-start(bf16[5,64,128]{2,1,0:T(8,128)(2,1)S(1)} %collective-permute-done.13.refs_6_) | copy-start | bytes 245764
  72.6 3.4 %copy-start.6 = (bf16[5,64,128]{2,1,0:T(8,128)(2,1)}, bf16[5,64,128]{2,1,0:T(8,128)(2,1)S(1)}, u32[]{:S(2)}) copy-start(bf16[5,64,128]{2,1,0:T(8,128)(2,1)S(1)} %collective-permute-done.14.refs_7_) | copy-start | bytes 245764
  72.6 3.4 %copy-start.7 = (bf16[5,64,128]{2,1,0:T(8,128)(2,1)}, bf16[5,64,128]{2,1,0:T(8,128)(2,1)S(1)}, u32[]{:S(2)}) copy-start(bf16[5,64,128]{2,1,0:T(8,128)(2,1)S(1)} %collective-permute-done.8.refs_1_) | copy-start | bytes 245764
  76.0 0.6 copy-start.8

commit v3 on v2

--- a/solution.py
+++ b/solution.py
@@ -12,7 +12,9 @@
 F32 = jnp.float32
 BF16 = jnp.bfloat16
 LANES = 128
-VMEM_BYTES = 58 * 1024 * 1024
+VMEM_BYTES = 52 * 1024 * 1024
+INTERACT_BYTES = 24 * 1024 * 1024
+SMALL_BYTES = 8 * 1024 * 1024
 
 
 def divisor(count, options):
@@ -188,30 +190,36 @@
         out_shape=outs,
         in_specs=[vmem] * reps,
         out_specs=[vmem] * len(outs),
-        compiler_params=pltpu.CompilerParams(vmem_limit_bytes=VMEM_BYTES),
+        compiler_params=pltpu.CompilerParams(vmem_limit_bytes=SMALL_BYTES),
         name="pack",
     )(*found)
 
 
 def join_kernel(*refs):
-    parts, out_ref = refs[:-1], refs[-1]
+    parts, out_ref, sem = refs[:-2], refs[-2], refs[-1]
     chips = len(parts)
     lanes = parts[0].shape[-1]
     chip = lax.axis_index("fld")
+    copies = []
     for k, part in enumerate(parts):
         at = pl.multiple_of(lax.rem(chip + chips - k, chips) * lanes, lanes)
-        out_ref[:, :, pl.ds(at, lanes)] = part[...]
+        copies.append(pltpu.make_async_copy(part, out_ref.at[:, :, pl.ds(at, lanes)], sem.at[k]))
+    for copy in copies:
+        copy.start()
+    for copy in copies:
+        copy.wait()
 
 
 def join(parts):
     per, width, lanes = parts[0].shape
-    vmem = pl.BlockSpec(memory_space=pltpu.VMEM)
+    anywhere = pl.BlockSpec(memory_space=pl.ANY)
     return pl.pallas_call(
         join_kernel,
         out_shape=jax.ShapeDtypeStruct((per, width, lanes * len(parts)), BF16),
-        in_specs=[vmem] * len(parts),
-        out_specs=vmem,
-        compiler_params=pltpu.CompilerParams(vmem_limit_bytes=VMEM_BYTES),
+        in_specs=[anywhere] * len(parts),
+        out_specs=anywhere,
+        scratch_shapes=[pltpu.SemaphoreType.DMA((len(parts),))],
+        compiler_params=pltpu.CompilerParams(vmem_limit_bytes=SMALL_BYTES),
         name="join",
     )(*parts)
 
@@ -399,7 +407,7 @@
         in_specs=[pl.BlockSpec(memory_space=pltpu.SMEM)] + [vmem] * (4 + len(given)),
         out_specs=[vmem] * len(given),
         scratch_shapes=scratch,
-        compiler_params=pltpu.CompilerParams(vmem_limit_bytes=VMEM_BYTES),
+        compiler_params=pltpu.CompilerParams(vmem_limit_bytes=INTERACT_BYTES),
         cost_estimate=pl.CostEstimate(
             flops=12_000_000_000, bytes_accessed=4_000_000, transcendentals=0
         ),
@@ -433,7 +441,7 @@
         out_shape=jax.ShapeDtypeStruct((1, lanes), F32),
         in_specs=[vmem] * (1 + len(blocks)),
         out_specs=vmem,
-        compiler_params=pltpu.CompilerParams(vmem_limit_bytes=VMEM_BYTES),
+        compiler_params=pltpu.CompilerParams(vmem_limit_bytes=SMALL_BYTES),
         cost_estimate=pl.CostEstimate(
             flops=1_000_000_000, bytes_accessed=1_000_000, transcendentals=0
         ),

time: 79.2 us -> 71 us (0.90)
  Pallas kernels: 34.3 us -> 26.9 us
  local copies, waits for them, and re-layouts: 2.73 us -> 0.94 us
  waiting for transfers between devices: 12.2 us -> 13.7 us
    pallas_call x1, Pallas kernels: 2.08 us -> 0.12 us  [pack(): pl.pallas_call(functools.partial(pack_kernel, sources=sources, reps=reps,...]
    ppermute x14, waiting for transfers between devices: 10.7 us -> 12.3 us  [swap(): lax.ppermute(blocks[k], 'fld', [(i, (i + k) % chips) for i in range(chips)])]
    pallas_call x1, Pallas kernels: 15.5 us -> 13.9 us  [lookup(): pl.pallas_call(functools.partial(lookup_kernel, step=step, slot_of=slot_o...]
    pallas_call x1, Pallas kernels: 2.2 us -> 0.89 us  [join(): pl.pallas_call(join_kernel, out_shape=jax.ShapeDtypeStruct((per, width, l...]
    pallas_call x1, Pallas kernels: 12.6 us -> 11.3 us  [interact(): pl.pallas_call(functools.partial(interact_kernel, chips=chips, group=grou...]
    unnamed x34 -> x14, local copies, waits for them, and re-layouts: 2.05 us -> 0.87 us
    pallas_call x1, Pallas kernels: 1.93 us -> 0.75 us  [logit(): pl.pallas_call(logit_kernel, out_shape=jax.ShapeDtypeStruct((1, lanes), F...]
  transfers between devices with their start and end apart: 15 -> 15, of which waited for: 7 -> 8; matrix products, arithmetic and copies ran while one was open for 1% -> 1% of each run, Pallas kernels for 2% -> 1%
where the time goes in v3:
time: 71 us; the launch traced here: 70.9 us
  starting transfers between devices  28.3 us (40%)
  Pallas kernels  26.9 us (38%)
  waiting for transfers between devices  13.7 us (19%)
  local copies, waits for them, and re-layouts  0.94 us (1%)
  between operations  0.73 us (1%)
    ppermute x14, starting transfers between devices, swap(): lax.ppermute(blocks[k], 'fld', [(i, (i + k) % chips) for i in range(chips)])  27.8 us
    pallas_call x1, Pallas kernels, lookup(): pl.pallas_call(functools.partial(lookup_kernel, step=step, slot_of=slot_o...  13.9 us
    ppermute x14, waiting for transfers between devices, swap(): lax.ppermute(blocks[k], 'fld', [(i, (i + k) % chips) for i in range(chips)])  12.3 us
    pallas_call x1, Pallas kernels, interact(): pl.pallas_call(functools.partial(interact_kernel, chips=chips, group=grou...  11.3 us
  transfers between devices with their start and end apart: 15, of which 8 were waited for; matrix products, arithmetic and copies ran while one was open for 1% of the time, Pallas kernels for 1%

profile of v3, /device:TPU:0, one launch (start us, length us, event | category | flops | bytes accessed | tf_op | source)
XLA Modules:
  0.0 70.9 jit_solution(16680225973106706457)
XLA Ops:
  0.6 0.0 copy-start
  0.7 0.8 %copy-done.1 = s32[2048,5]{0,1:T(8,128)S(1)} copy-done((s32[2048,5]{0,1:T(8,128)S(1)}, s32[2048,5]{0,1:T(8,128)}, u32[]{:S(2)}) %copy-start.1) | copy-done | bytes 40984
  1.5 13.9 %shard_map.95 = (bf16[8,3,64,128]{3,2,1,0:T(8,128)(2,1)S(1)}, bf16[8,3,64,128]{3,2,1,0:T(8,128)(2,1)S(1)}) custom-call(s32[5,2048]{1,0:T(8,128)S(1)} %bitcast.4, bf16[64,163840]{1,0:T(8,128)(2,1)} %bitcast.6), custom_call_target="tpu_custom_call" | custom-call | flops 35999997952 | bytes 20971520 | tf_op jit(solution)/shard_map/pallas_call | solution.py:134
  15.4 0.5 collective-permute-start
  15.9 1.3 %collective-permute-done.refs_1_ = bf16[8,3,64,128]{3,2,1,0:T(8,128)(2,1)S(1)} collective-permute-done((bf16[8,3,64,128]{3,2,1,0:T(8,128)(2,1)S(1)}, bf16[8,3,64,128]{3,2,1,0:T(8,128)(2,1)S(1)}, u32[]{:S(2)}, u32[]{:S(2)}) %collective-permute-start) | collective-permute-done | bytes 393248 | tf_op jit(solution)/shard_map/ppermute | solution.py:499
  17.2 0.1 pack.1
  17.4 3.0 %collective-permute-start.1 = (bf16[5,64,128]{2,1,0:T(8,128)(2,1)S(1)}, bf16[5,64,128]{2,1,0:T(8,128)(2,1)S(1)}, u32[]{:S(2)}, u32[]{:S(2)}) collective-permute-start(bf16[5,64,128]{2,1,0:T(8,128)(2,1)S(1)} %get-tuple-element.23), channel_id=1, source_target_pairs={{0,2},{2,4},{4,6},{6,8},{8,10},{10,12},{12,14},{14,0},{1,3},{3,5},... | collective-permute-start | bytes 245768 | tf_op jit(solution)/shard_map/ppermute | solution.py:231
  20.3 1.6 %collective-permute-start.2 = (bf16[5,64,128]{2,1,0:T(8,128)(2,1)S(1)}, bf16[5,64,128]{2,1,0:T(8,128)(2,1)S(1)}, u32[]{:S(2)}, u32[]{:S(2)}) collective-permute-start(bf16[5,64,128]{2,1,0:T(8,128)(2,1)S(1)} %get-tuple-element.24), channel_id=1, source_target_pairs={{0,4},{2,6},{4,8},{6,10},{8,12},{10,14},{12,0},{14,2},{1,5},{3,7},... | collective-permute-start | bytes 245768 | tf_op jit(solution)/shard_map/ppermute | solution.py:231
  21.9 2.6 %collective-permute-start.3 = (bf16[5,64,128]{2,1,0:T(8,128)(2,1)S(1)}, bf16[5,64,128]{2,1,0:T(8,128)(2,1)S(1)}, u32[]{:S(2)}, u32[]{:S(2)}) collective-permute-start(bf16[5,64,128]{2,1,0:T(8,128)(2,1)S(1)} %get-tuple-element.25), channel_id=1, source_target_pairs={{0,6},{2,8},{4,10},{6,12},{8,14},{10,0},{12,2},{14,4},{1,7},{3,9},... | collective-permute-start | bytes 245768 | tf_op jit(solution)/shard_map/ppermute | solution.py:231
  24.5 1.2 %collective-permute-start.4 = (bf16[5,64,128]{2,1,0:T(8,128)(2,1)S(1)}, bf16[5,64,128]{2,1,0:T(8,128)(2,1)S(1)}, u32[]{:S(2)}, u32[]{:S(2)}) collective-permute-start(bf16[5,64,128]{2,1,0:T(8,128)(2,1)S(1)} %get-tuple-element.26), channel_id=1, source_target_pairs={{0,8},{2,10},{4,12},{6,14},{8,0},{10,2},{12,4},{14,6},{1,9},{3,11}... | collective-permute-start | bytes 245768 | tf_op jit(solution)/shard_map/ppermute | solution.py:231
  25.7 2.6 %collective-permute-start.5 = (bf16[5,64,128]{2,1,0:T(8,128)(2,1)S(1)}, bf16[5,64,128]{2,1,0:T(8,128)(2,1)S(1)}, u32[]{:S(2)}, u32[]{:S(2)}) collective-permute-start(bf16[5,64,128]{2,1,0:T(8,128)(2,1)S(1)} %get-tuple-element.27), channel_id=1, source_target_pairs={{0,10},{2,12},{4,14},{6,0},{8,2},{10,4},{12,6},{14,8},{1,11},{3,13... | collective-permute-start | bytes 245768 | tf_op jit(solution)/shard_map/ppermute | solution.py:231
  28.3 0.0 collective-permute-done.1.refs_1_
  28.3 1.3 %collective-permute-start.6 = (bf16[5,64,128]{2,1,0:T(8,128)(2,1)S(1)}, bf16[5,64,128]{2,1,0:T(8,128)(2,1)S(1)}, u32[]{:S(2)}, u32[]{:S(2)}) collective-permute-start(bf16[5,64,128]{2,1,0:T(8,128)(2,1)S(1)} %get-tuple-element.28), channel_id=1, source_target_pairs={{0,12},{2,14},{4,0},{6,2},{8,4},{10,6},{12,8},{14,10},{1,13},{3,15... | collective-permute-start | bytes 245768 | tf_op jit(solution)/shard_map/ppermute | solution.py:231
  29.7 1.4 %collective-permute-start.7 = (bf16[5,64,128]{2,1,0:T(8,128)(2,1)S(1)}, bf16[5,64,128]{2,1,0:T(8,128)(2,1)S(1)}, u32[]{:S(2)}, u32[]{:S(2)}) collective-permute-start(bf16[5,64,128]{2,1,0:T(8,128)(2,1)S(1)} %get-tuple-element.29), channel_id=1, source_target_pairs={{0,14},{2,0},{4,2},{6,4},{8,6},{10,8},{12,10},{14,12},{1,15},{3,1}... | collective-permute-start | bytes 245768 | tf_op jit(solution)/shard_map/ppermute | solution.py:231
  31.1 2.2 %collective-permute-done.3.refs_3_ = bf16[5,64,128]{2,1,0:T(8,128)(2,1)S(1)} collective-permute-done((bf16[5,64,128]{2,1,0:T(8,128)(2,1)S(1)}, bf16[5,64,128]{2,1,0:T(8,128)(2,1)S(1)}, u32[]{:S(2)}, u32[]{:S(2)}) %collective-permute-start.3) | collective-permute-done | bytes 81952 | tf_op jit(solution)/shard_map/ppermute | solution.py:231
  33.3 0.7 %collective-permute-done.4.refs_4_ = bf16[5,64,128]{2,1,0:T(8,128)(2,1)S(1)} collective-permute-done((bf16[5,64,128]{2,1,0:T(8,128)(2,1)S(1)}, bf16[5,64,128]{2,1,0:T(8,128)(2,1)S(1)}, u32[]{:S(2)}, u32[]{:S(2)}) %collective-permute-start.4) | collective-permute-done | bytes 81952 | tf_op jit(solution)/shard_map/ppermute | solution.py:231
  34.1 1.9 %collective-permute-done.6.refs_6_ = bf16[5,64,128]{2,1,0:T(8,128)(2,1)S(1)} collective-permute-done((bf16[5,64,128]{2,1,0:T(8,128)(2,1)S(1)}, bf16[5,64,128]{2,1,0:T(8,128)(2,1)S(1)}, u32[]{:S(2)}, u32[]{:S(2)}) %collective-permute-start.6) | collective-permute-done | bytes 81952 | tf_op jit(solution)/shard_map/ppermute | solution.py:231
  36.0 11.3 %interact.1 = (bf16[5,64,128]{2,1,0:T(8,128)(2,1)S(1)}, bf16[5,64,128]{2,1,0:T(8,128)(2,1)S(1)}, bf16[5,64,128]{2,1,0:T(8,128)(2,1)S(1)}, bf16[5,64,128]{2,1,0:T...) custom-call(s32[40]{0:T(128)S(1)} %copy-done.6, ...), custom_call_target="tpu_custom_call" | custom-call | flops 12000000000 | bytes 4000000 | tf_op jit(solution)/shard_map/interact/pallas_call | solution.py:404
  47.3 4.7 %collective-permute-start.10 = (bf16[5,64,128]{2,1,0:T(8,128)(2,1)S(1)}, bf16[5,64,128]{2,1,0:T(8,128)(2,1)S(1)}, u32[]{:S(2)}, u32[]{:S(2)}) collective-permute-start(bf16[5,64,128]{2,1,0:T(8,128)(2,1)S(1)} %get-tuple-element.33.refs_3_), channel_id=1, source_target_pairs={{0,6},{2,8},{4,10},{6,12},{8,14},{10,0},{12,2},{14,4},{1,7},{3,9},... | collective-permute-start | bytes 245768 | tf_op jit(solution)/shard_map/ppermute | solution.py:231
  52.1 1.3 %collective-permute-start.11 = (bf16[5,64,128]{2,1,0:T(8,128)(2,1)S(1)}, bf16[5,64,128]{2,1,0:T(8,128)(2,1)S(1)}, u32[]{:S(2)}, u32[]{:S(2)}) collective-permute-start(bf16[5,64,128]{2,1,0:T(8,128)(2,1)S(1)} %get-tuple-element.34.refs_4_), channel_id=1, source_target_pairs={{0,8},{2,10},{4,12},{6,14},{8,0},{10,2},{12,4},{14,6},{1,9},{3,11}... | collective-permute-start | bytes 245768 | tf_op jit(solution)/shard_map/ppermute | solution.py:231
  53.4 0.3 fusion
  53.7 0.1 reshape.18.w_ref
  53.7 1.1 %collective-permute-start.12 = (bf16[5,64,128]{2,1,0:T(8,128)(2,1)S(1)}, bf16[5,64,128]{2,1,0:T(8,128)(2,1)S(1)}, u32[]{:S(2)}, u32[]{:S(2)}) collective-permute-start(bf16[5,64,128]{2,1,0:T(8,128)(2,1)S(1)} %get-tuple-element.35.refs_5_), channel_id=1, source_target_pairs={{0,10},{2,12},{4,14},{6,0},{8,2},{10,4},{12,6},{14,8},{1,11},{3,13... | collective-permute-start | bytes 245768 | tf_op jit(solution)/shard_map/ppermute | solution.py:231
  54.8 1.5 %collective-permute-start.13 = (bf16[5,64,128]{2,1,0:T(8,128)(2,1)S(1)}, bf16[5,64,128]{2,1,0:T(8,128)(2,1)S(1)}, u32[]{:S(2)}, u32[]{:S(2)}) collective-permute-start(bf16[5,64,128]{2,1,0:T(8,128)(2,1)S(1)} %get-tuple-element.36.refs_6_), channel_id=1, source_target_pairs={{0,12},{2,14},{4,0},{6,2},{8,4},{10,6},{12,8},{14,10},{1,13},{3,15... | collective-permute-start | bytes 245768 | tf_op jit(solution)/shard_map/ppermute | solution.py:231
  56.3 1.4 %collective-permute-start.14 = (bf16[5,64,128]{2,1,0:T(8,128)(2,1)S(1)}, bf16[5,64,128]{2,1,0:T(8,128)(2,1)S(1)}, u32[]{:S(2)}, u32[]{:S(2)}) collective-permute-start(bf16[5,64,128]{2,1,0:T(8,128)(2,1)S(1)} %get-tuple-element.37.refs_7_), channel_id=1, source_target_pairs={{0,14},{2,0},{4,2},{6,4},{8,6},{10,8},{12,10},{14,12},{1,15},{3,1}... | collective-permute-start | bytes 245768 | tf_op jit(solution)/shard_map/ppermute | solution.py:231
  57.7 1.2 %collective-permute-done.10.refs_3_ = bf16[5,64,128]{2,1,0:T(8,128)(2,1)S(1)} collective-permute-done((bf16[5,64,128]{2,1,0:T(8,128)(2,1)S(1)}, bf16[5,64,128]{2,1,0:T(8,128)(2,1)S(1)}, u32[]{:S(2)}, u32[]{:S(2)}) %collective-permute-start.10) | collective-permute-done | bytes 81952 | tf_op jit(solution)/shard_map/ppermute | solution.py:231
  58.9 1.8 %collective-permute-done.11.refs_4_ = bf16[5,64,128]{2,1,0:T(8,128)(2,1)S(1)} collective-permute-done((bf16[5,64,128]{2,1,0:T(8,128)(2,1)S(1)}, bf16[5,64,128]{2,1,0:T(8,128)(2,1)S(1)}, u32[]{:S(2)}, u32[]{:S(2)}) %collective-permute-start.11) | collective-permute-done | bytes 81952 | tf_op jit(solution)/shard_map/ppermute | solution.py:231
  60.7 4.0 %collective-permute-start.9 = (bf16[5,64,128]{2,1,0:T(8,128)(2,1)S(1)}, bf16[5,64,128]{2,1,0:T(8,128)(2,1)S(1)}, u32[]{:S(2)}, u32[]{:S(2)}) collective-permute-start(bf16[5,64,128]{2,1,0:T(8,128)(2,1)S(1)} %get-tuple-element.32.refs_2_), channel_id=1, source_target_pairs={{0,4},{2,6},{4,8},{6,10},{8,12},{10,14},{12,0},{14,2},{1,5},{3,7},... | collective-permute-start | bytes 245768 | tf_op jit(solution)/shard_map/ppermute | solution.py:231
  64.7 0.7 %logit.1 = f32[1,128]{1,0:T(1,128)} custom-call(f32[8,320]{1,0:T(8,128)S(1)} %reshape.18.w_ref, bf16[5,64,128]{2,1,0:T(8,128)(2,1)S(1)} %get-tuple-element.30.refs_0_, bf16[5,64,128]{2,1,0:T(8,128)(2,1)S(1)} %get-tuple-element.31.refs_1_, bf16[5,64,128]{2,1,0:T(8,128)(2,1)S(1)} %get-tuple-element.32.refs_2_, ...), custom_call_target="tpu_custom_call" | custom-call | flops 1000000000 | bytes 1000000 | tf_op jit(solution)/shard_map/logit/pallas_call | solution.py:439
  65.5 0.6 collective-permute-done.8.refs_1_
  66.1 3.9 %collective-permute-done.9.refs_2_ = bf16[5,64,128]{2,1,0:T(8,128)(2,1)S(1)} collective-permute-done((bf16[5,64,128]{2,1,0:T(8,128)(2,1)S(1)}, bf16[5,64,128]{2,1,0:T(8,128)(2,1)S(1)}, u32[]{:S(2)}, u32[]{:S(2)}) %collective-permute-start.9) | collective-permute-done | bytes 81952 | tf_op jit(solution)/shard_map/ppermute | solution.py:231
  70.0 0.9 %join.1 = bf16[5,64,1024]{2,1,0:T(8,128)(2,1)} custom-call(bf16[5,64,128]{2,1,0:T(8,128)(2,1)S(1)} %get-tuple-element.30.refs_0_, bf16[5,64,128]{2,1,0:T(8,128)(2,1)S(1)} %collective-permute-done.8.refs_1_, bf16[5,64,128]{2,1,0:T(8,128)(2,1)S(1)} %collective-permute-done.9.refs_2_, bf16[5,64,128]{2,1,0:T(8,128)(2,1)S(1)} %collective-permute-done.10.refs_3_, ...), custom_call_target="tpu_custom_call" | custom-call | tf_op jit(solution)/shard_map/join/pallas_call | solution.py:216
  (20 shorter events, 0.1 us)
Async XLA Ops:
  0.6 52.8 %copy-start = (f32[40,64]{1,0:T(8,128)S(1)}, f32[40,64]{1,0:T(8,128)}, u32[]{:S(2)}) copy-start(f32[40,64]{1,0:T(8,128)} %param.15) | copy-start | bytes 30724
  0.6 0.8 %copy-start.1 = (s32[2048,5]{0,1:T(8,128)S(1)}, s32[2048,5]{0,1:T(8,128)}, u32[]{:S(2)}) copy-start(s32[2048,5]{0,1:T(8,128)} %param.8) | copy-start | bytes 122884
  1.5 34.5 %copy-start.2 = (bf16[2,64,64]{2,1,0:T(8,128)(2,1)S(1)}, bf16[2,64,64]{2,1,0:T(8,128)(2,1)}, u32[]{:S(2)}) copy-start(bf16[2,64,64]{2,1,0:T(8,128)(2,1)} %wq_ref.1) | copy-start | bytes 49156
  1.5 34.5 %copy-start.3 = (bf16[2,64,64]{2,1,0:T(8,128)(2,1)S(1)}, bf16[2,64,64]{2,1,0:T(8,128)(2,1)}, u32[]{:S(2)}) copy-start(bf16[2,64,64]{2,1,0:T(8,128)(2,1)} %wk_ref.1) | copy-start | bytes 49156
  1.5 34.5 %copy-start.4 = (bf16[2,64,64]{2,1,0:T(8,128)(2,1)S(1)}, bf16[2,64,64]{2,1,0:T(8,128)(2,1)}, u32[]{:S(2)}) copy-start(bf16[2,64,64]{2,1,0:T(8,128)(2,1)} %wv_ref.1) | copy-start | bytes 49156
  1.5 34.5 %copy-start.5 = (bf16[2,64,64]{2,1,0:T(8,128)(2,1)S(1)}, bf16[2,64,64]{2,1,0:T(8,128)(2,1)}, u32[]{:S(2)}) copy-start(bf16[2,64,64]{2,1,0:T(8,128)(2,1)} %wr_ref.1) | copy-start | bytes 49156
  1.5 34.5 %copy-start.6 = (s32[40]{0:T(128)S(1)}, s32[40]{0:T(128)}, u32[]{:S(2)}) copy-start(s32[40]{0:T(128)} %place_ref.1) | copy-start | bytes 484
  15.4 1.9 %collective-permute-start = (bf16[8,3,64,128]{3,2,1,0:T(8,128)(2,1)S(1)}, bf16[8,3,64,128]{3,2,1,0:T(8,128)(2,1)S(1)}, u32[]{:S(2)}, u32[]{:S(2)}) collective-permute-start(bf16[8,3,64,128]{3,2,1,0:T(8,128)(2,1)S(1)} %get-tuple-element.21), channel_id=1, source_target_pairs={{0,1},{1,0},{2,3},{3,2},{4,5},{5,4},{6,7},{7,6},{8,9},{9,8},{10,11... | collective-permute-start | bytes 1179656 | tf_op jit(solution)/shard_map/ppermute | solution.py:499
  17.4 11.0 %collective-permute-start.1 = (bf16[5,64,128]{2,1,0:T(8,128)(2,1)S(1)}, bf16[5,64,128]{2,1,0:T(8,128)(2,1)S(1)}, u32[]{:S(2)}, u32[]{:S(2)}) collective-permute-start(bf16[5,64,128]{2,1,0:T(8,128)(2,1)S(1)} %get-tuple-element.23), channel_id=1, source_target_pairs={{0,2},{2,4},{4,6},{6,8},{8,10},{10,12},{12,14},{14,0},{1,3},{3,5},... | collective-permute-start | bytes 245768 | tf_op jit(solution)/shard_map/ppermute | solution.py:231
  20.3 9.3 %collective-permute-start.2 = (bf16[5,64,128]{2,1,0:T(8,128)(2,1)S(1)}, bf16[5,64,128]{2,1,0:T(8,128)(2,1)S(1)}, u32[]{:S(2)}, u32[]{:S(2)}) collective-permute-start(bf16[5,64,128]{2,1,0:T(8,128)(2,1)S(1)} %get-tuple-element.24), channel_id=1, source_target_pairs={{0,4},{2,6},{4,8},{6,10},{8,12},{10,14},{12,0},{14,2},{1,5},{3,7},... | collective-permute-start | bytes 245768 | tf_op jit(solution)/shard_map/ppermute | solution.py:231
  21.9 11.4 %collective-permute-start.3 = (bf16[5,64,128]{2,1,0:T(8,128)(2,1)S(1)}, bf16[5,64,128]{2,1,0:T(8,128)(2,1)S(1)}, u32[]{:S(2)}, u32[]{:S(2)}) collective-permute-start(bf16[5,64,128]{2,1,0:T(8,128)(2,1)S(1)} %get-tuple-element.25), channel_id=1, source_target_pairs={{0,6},{2,8},{4,10},{6,12},{8,14},{10,0},{12,2},{14,4},{1,7},{3,9},... | collective-permute-start | bytes 245768 | tf_op jit(solution)/shard_map/ppermute | solution.py:231
  24.5 9.6 %collective-permute-start.4 = (bf16[5,64,128]{2,1,0:T(8,128)(2,1)S(1)}, bf16[5,64,128]{2,1,0:T(8,128)(2,1)S(1)}, u32[]{:S(2)}, u32[]{:S(2)}) collective-permute-start(bf16[5,64,128]{2,1,0:T(8,128)(2,1)S(1)} %get-tuple-element.26), channel_id=1, source_target_pairs={{0,8},{2,10},{4,12},{6,14},{8,0},{10,2},{12,4},{14,6},{1,9},{3,11}... | collective-permute-start | bytes 245768 | tf_op jit(solution)/shard_map/ppermute | solution.py:231
  25.7 8.4 %collective-permute-start.5 = (bf16[5,64,128]{2,1,0:T(8,128)(2,1)S(1)}, bf16[5,64,128]{2,1,0:T(8,128)(2,1)S(1)}, u32[]{:S(2)}, u32[]{:S(2)}) collective-permute-start(bf16[5,64,128]{2,1,0:T(8,128)(2,1)S(1)} %get-tuple-element.27), channel_id=1, source_target_pairs={{0,10},{2,12},{4,14},{6,0},{8,2},{10,4},{12,6},{14,8},{1,11},{3,13... | collective-permute-start | bytes 245768 | tf_op jit(solution)/shard_map/ppermute | solution.py:231
  28.3 7.7 %collective-permute-start.6 = (bf16[5,64,128]{2,1,0:T(8,128)(2,1)S(1)}, bf16[5,64,128]{2,1,0:T(8,128)(2,1)S(1)}, u32[]{:S(2)}, u32[]{:S(2)}) collective-permute-start(bf16[5,64,128]{2,1,0:T(8,128)(2,1)S(1)} %get-tuple-element.28), channel_id=1, source_target_pairs={{0,12},{2,14},{4,0},{6,2},{8,4},{10,6},{12,8},{14,10},{1,13},{3,15... | collective-permute-start | bytes 245768 | tf_op jit(solution)/shard_map/ppermute | solution.py:231
  29.7 6.3 %collective-permute-start.7 = (bf16[5,64,128]{2,1,0:T(8,128)(2,1)S(1)}, bf16[5,64,128]{2,1,0:T(8,128)(2,1)S(1)}, u32[]{:S(2)}, u32[]{:S(2)}) collective-permute-start(bf16[5,64,128]{2,1,0:T(8,128)(2,1)S(1)} %get-tuple-element.29), channel_id=1, source_target_pairs={{0,14},{2,0},{4,2},{6,4},{8,6},{10,8},{12,10},{14,12},{1,15},{3,1}... | collective-permute-start | bytes 245768 | tf_op jit(solution)/shard_map/ppermute | solution.py:231
  47.3 11.6 %collective-permute-start.10 = (bf16[5,64,128]{2,1,0:T(8,128)(2,1)S(1)}, bf16[5,64,128]{2,1,0:T(8,128)(2,1)S(1)}, u32[]{:S(2)}, u32[]{:S(2)}) collective-permute-start(bf16[5,64,128]{2,1,0:T(8,128)(2,1)S(1)} %get-tuple-element.33.refs_3_), channel_id=1, source_target_pairs={{0,6},{2,8},{4,10},{6,12},{8,14},{10,0},{12,2},{14,4},{1,7},{3,9},... | collective-permute-start | bytes 245768 | tf_op jit(solution)/shard_map/ppermute | solution.py:231
  52.1 8.6 %collective-permute-start.11 = (bf16[5,64,128]{2,1,0:T(8,128)(2,1)S(1)}, bf16[5,64,128]{2,1,0:T(8,128)(2,1)S(1)}, u32[]{:S(2)}, u32[]{:S(2)}) collective-permute-start(bf16[5,64,128]{2,1,0:T(8,128)(2,1)S(1)} %get-tuple-element.34.refs_4_), channel_id=1, source_target_pairs={{0,8},{2,10},{4,12},{6,14},{8,0},{10,2},{12,4},{14,6},{1,9},{3,11}... | collective-permute-start | bytes 245768 | tf_op jit(solution)/shard_map/ppermute | solution.py:231
  53.7 11.7 %collective-permute-start.12 = (bf16[5,64,128]{2,1,0:T(8,128)(2,1)S(1)}, bf16[5,64,128]{2,1,0:T(8,128)(2,1)S(1)}, u32[]{:S(2)}, u32[]{:S(2)}) collective-permute-start(bf16[5,64,128]{2,1,0:T(8,128)(2,1)S(1)} %get-tuple-element.35.refs_5_), channel_id=1, source_target_pairs={{0,10},{2,12},{4,14},{6,0},{8,2},{10,4},{12,6},{14,8},{1,11},{3,13... | collective-permute-start | bytes 245768 | tf_op jit(solution)/shard_map/ppermute | solution.py:231
  54.8 10.7 %collective-permute-start.13 = (bf16[5,64,128]{2,1,0:T(8,128)(2,1)S(1)}, bf16[5,64,128]{2,1,0:T(8,128)(2,1)S(1)}, u32[]{:S(2)}, u32[]{:S(2)}) collective-permute-start(bf16[5,64,128]{2,1,0:T(8,128)(2,1)S(1)} %get-tuple-element.36.refs_6_), channel_id=1, source_target_pairs={{0,12},{2,14},{4,0},{6,2},{8,4},{10,6},{12,8},{14,10},{1,13},{3,15... | collective-permute-start | bytes 245768 | tf_op jit(solution)/shard_map/ppermute | solution.py:231
  56.3 9.2 %collective-permute-start.14 = (bf16[5,64,128]{2,1,0:T(8,128)(2,1)S(1)}, bf16[5,64,128]{2,1,0:T(8,128)(2,1)S(1)}, u32[]{:S(2)}, u32[]{:S(2)}) collective-permute-start(bf16[5,64,128]{2,1,0:T(8,128)(2,1)S(1)} %get-tuple-element.37.refs_7_), channel_id=1, source_target_pairs={{0,14},{2,0},{4,2},{6,4},{8,6},{10,8},{12,10},{14,12},{1,15},{3,1}... | collective-permute-start | bytes 245768 | tf_op jit(solution)/shard_map/ppermute | solution.py:231
  58.9 7.1 %collective-permute-start.8 = (bf16[5,64,128]{2,1,0:T(8,128)(2,1)S(1)}, bf16[5,64,128]{2,1,0:T(8,128)(2,1)S(1)}, u32[]{:S(2)}, u32[]{:S(2)}) collective-permute-start(bf16[5,64,128]{2,1,0:T(8,128)(2,1)S(1)} %get-tuple-element.31.refs_1_), channel_id=1, source_target_pairs={{0,2},{2,4},{4,6},{6,8},{8,10},{10,12},{12,14},{14,0},{1,3},{3,5},... | collective-permute-start | bytes 245768 | tf_op jit(solution)/shard_map/ppermute | solution.py:231
  60.7 9.3 %collective-permute-start.9 = (bf16[5,64,128]{2,1,0:T(8,128)(2,1)S(1)}, bf16[5,64,128]{2,1,0:T(8,128)(2,1)S(1)}, u32[]{:S(2)}, u32[]{:S(2)}) collective-permute-start(bf16[5,64,128]{2,1,0:T(8,128)(2,1)S(1)} %get-tuple-element.32.refs_2_), channel_id=1, source_target_pairs={{0,4},{2,6},{4,8},{6,10},{8,12},{10,14},{12,0},{14,2},{1,5},{3,7},... | collective-permute-start | bytes 245768 | tf_op jit(solution)/shard_map/ppermute | solution.py:231

commit v4 on v3

--- a/solution.py
+++ b/solution.py
@@ -7,6 +7,7 @@
 from jax.experimental import pallas as pl
 from jax.experimental.pallas import tpu as pltpu
 from jax.sharding import PartitionSpec as P
+
 
 HEADS = 2
 F32 = jnp.float32
@@ -32,8 +33,8 @@
 def lookup_kernel(
     ids_ref, tab_ref, *refs, step, slot_of, shift_of, bounds_of, owned
 ):
-    outs = refs[:-8]
-    land, tab, stage, lines, odd_ref, row_ref, sem, row_sem = refs[-8:]
+    outs = refs[:-10]
+    land, tab, stage, ids_s, lines, odd_ref, row_ref, sem, ids_sem, row_sem = refs[-10:]
     chips, slots, width, lanes = outs[0].shape
     reps = len(bounds_of[0])
     blocks = chips * reps
@@ -57,16 +58,19 @@
         def _():
             fetch(first + i).start()
 
+    ids_copy = pltpu.make_async_copy(ids_ref, ids_s, ids_sem)
+    ids_copy.start()
     tab[pl.ds(spare, 8), :] = jnp.zeros((8, 2 * width), F32)
+    ids_copy.wait()
     for j in range(slots):
         shift = by_rep(shift_of[j])
         for b in range(blocks):
             to_rep = lax.rem(rep + b // chips, reps)
             to_chip = lax.rem(chip + b % chips, chips)
             at = pl.ds(pl.multiple_of((to_rep * chips + to_chip) * lanes, lanes), lanes)
-            rows = ids_ref[slot_of[j][0] : slot_of[j][0] + 1, at]
+            rows = ids_s[slot_of[j][0] : slot_of[j][0] + 1, at]
             for r, slot in enumerate(slot_of[j][1:], 1):
-                rows = jnp.where(rep == r, ids_ref[slot : slot + 1, at], rows)
+                rows = jnp.where(rep == r, ids_s[slot : slot + 1, at], rows)
             rows = rows + shift
             here = (rows >= 0) & (rows < owned)
             rows = rows - first * step
@@ -75,7 +79,6 @@
             odd_ref[pl.ds(j * blocks + b, 1), :] = (rows >> 7) & 1
     rows_copy = pltpu.make_async_copy(lines, row_ref, row_sem)
     rows_copy.start()
-    rows_copy.wait()
     for j in range(slots):
 
         def chunk(c, carry):
@@ -100,6 +103,8 @@
             return carry
 
         lax.fori_loop(bounds[j], bounds[j + 1], chunk, 0)
+        if j == 0:
+            rows_copy.wait()
 
         def some_blocks(i, carry, j=j, out_ref=None, ahead=0):
             def some(n, carry):
@@ -130,7 +135,6 @@
     blocks = chips * reps
     batch = divisor(chips, (4, 2, 1))
     vmem = pl.BlockSpec(memory_space=pltpu.VMEM)
-    anywhere = pl.BlockSpec(memory_space=pl.ANY)
     return pl.pallas_call(
         functools.partial(
             lookup_kernel,
@@ -141,16 +145,18 @@
             owned=owned,
         ),
         out_shape=[jax.ShapeDtypeStruct((chips, slots, width, LANES), BF16)] * reps,
-        in_specs=[vmem, anywhere],
+        in_specs=[pl.BlockSpec(memory_space=pltpu.HBM)] * 2,
         out_specs=[vmem] * reps,
         scratch_shapes=[
             pltpu.VMEM((buffers, width, step), BF16),
             pltpu.VMEM((most // 2 + 8, 2 * width), F32),
             pltpu.VMEM((batch * LANES, 2 * width), F32),
+            pltpu.VMEM(ids.shape, jnp.int32),
             pltpu.VMEM((slots * blocks, LANES), jnp.int32),
             pltpu.VMEM((slots * blocks, LANES), jnp.int32),
             pltpu.SMEM((slots * blocks, LANES), jnp.int32),
             pltpu.SemaphoreType.DMA((buffers,)),
+            pltpu.SemaphoreType.DMA,
             pltpu.SemaphoreType.DMA,
         ],
         compiler_params=pltpu.CompilerParams(vmem_limit_bytes=VMEM_BYTES),
@@ -228,7 +234,8 @@
     chips = len(blocks)
     out = [blocks[0]]
     for k in range(1, chips):
-        out.append(lax.ppermute(blocks[k], "fld", [(i, (i + k) % chips) for i in range(chips)]))
+        route = [(i, (i + k) % chips) for i in range(chips)]
+        out.append(lax.ppermute(blocks[k], "fld", route))
     return out
 
 
@@ -332,10 +339,32 @@
     return jnp.concatenate([ref[l].astype(F32).T.astype(BF16) for ref in refs], axis=0)
 
 
-def interact_kernel(place_ref, wq_ref, wk_ref, wv_ref, wr_ref, *refs, chips, group, fields):
-    q_s, kt_s, k_s, v_s, r_s, a_s, x_s, h_s = refs[-8:]
-    blocks = (len(refs) - 8) // 2
-    ins, outs = refs[:blocks], refs[blocks : 2 * blocks]
+def shifts_of(chips, group):
+    order = sorted(range(chips), key=lambda k: abs(k - chips / 2))
+    groups = [order[n : n + group] for n in range(0, chips, group)]
+    half = -(-len(groups) // 2)
+    return groups[:half], groups[half:]
+
+
+def last_layer(groups, outs, q_s, k_s, v_s, r_s, a_s, chips, group):
+    per = outs[0].shape[0]
+    size = outs[0].shape[1] // HEADS
+    chip = lax.axis_index("fld")
+    for n, ks in enumerate(groups):
+
+        def field_of(i, u, ks=ks):
+            return lax.rem(chip + ks[u], chips) * per + i
+
+        def store(i, u, at, out, n=n):
+            outs[n * group + u][i, at : at + size, :] = out
+
+        attend(q_s, k_s, v_s, r_s, a_s, store, field_of, per * group, group)
+
+
+def interact_kernel(place_ref, wq_ref, wk_ref, wv_ref, wr_ref, *refs, chips, group, fields, single):
+    a_s, kt_s, x_s, h_s = refs[-4:]
+    ins, outs, (q_s, k_s, v_s, r_s) = refs[: 1 if single else chips], refs[:-8], refs[-8:-4]
+    outs = outs[len(ins) :]
     per, width, lanes = ins[0].shape[-3:]
     layers = wq_ref.shape[0]
     size = width // HEADS
@@ -349,7 +378,7 @@
     for k in range(chips):
         back = lax.rem(chip + chips - k, chips)
         for s in range(per):
-            x_s[back * per + s] = ins[k][s] if blocks == chips else ins[0][back, s]
+            x_s[back * per + s] = ins[0][back, s] if single else ins[k][s]
 
     for l in range(layers):
         if l == 0:
@@ -363,16 +392,9 @@
                 h_s[i * group + u, at : at + size, :] = out
 
             attend(q_s, k_s, v_s, r_s, a_s, store, in_order, fields, group)
-        elif blocks == chips:
-            for low in range(0, chips, group):
-
-                def field_of(i, u, low=low):
-                    return lax.rem(chip + low + u, chips) * per + i
-
-                def store(i, u, at, out, low=low):
-                    outs[low + u][i, at : at + size, :] = out
-
-                attend(q_s, k_s, v_s, r_s, a_s, store, field_of, per * group, group)
+        elif not single:
+            groups = shifts_of(chips, group)[0]
+            last_layer(groups, outs, q_s, k_s, v_s, r_s, a_s, chips, group)
         else:
             for k in range(chips if not whole else 0):
                 for s in range(per):
@@ -386,26 +408,43 @@
             attend(q_s, k_s, v_s, r_s, a_s, store, in_order, fields, group)
 
 
-def interact(place, given, chips, weights, fields):
+def rest_kernel(q_s, k_s, v_s, r_s, *refs, chips, group):
+    groups = shifts_of(chips, group)[1]
+    last_layer(groups, refs[:-1], q_s, k_s, v_s, r_s, refs[-1], chips, group)
+
+
+def interact(place, given, chips, weights, fields, single):
     per, width, lanes = given[0].shape[-3:]
     group = divisor(math.gcd(fields, chips), (4, 2, 1))
-    wide = pltpu.VMEM((fields, width, lanes), F32)
     vmem = pl.BlockSpec(memory_space=pltpu.VMEM)
+    wide = ((fields, width, lanes), F32)
+    state = [
+        wide,
+        ((width // 2, 2 * fields, lanes), BF16),
+        ((fields // 2, 2 * width, lanes), BF16),
+        wide,
+    ]
+    attention = pltpu.VMEM((group * fields, lanes), F32)
     scratch = [
-        wide,
+        attention,
         pltpu.VMEM((width * fields, lanes), F32),
-        pltpu.VMEM((width // 2, 2 * fields, lanes), BF16),
-        pltpu.VMEM((fields // 2, 2 * width, lanes), BF16),
-        wide,
-        pltpu.VMEM((group * fields, lanes), F32),
         pltpu.VMEM((chips * per, width, lanes), BF16),
         pltpu.VMEM((fields, width, lanes), BF16),
     ]
-    return pl.pallas_call(
-        functools.partial(interact_kernel, chips=chips, group=group, fields=fields),
-        out_shape=[jax.ShapeDtypeStruct(x.shape, BF16) for x in given],
+    first, second = ([], []) if single else shifts_of(chips, group)
+    first, second = sum(first, []), sum(second, [])
+    made = [jax.ShapeDtypeStruct(given[0].shape, BF16)] * (1 if single else len(first))
+    if second:
+        made = made + [jax.ShapeDtypeStruct(*x) for x in state]
+    else:
+        scratch = [pltpu.VMEM(*x) for x in state] + scratch
+    done = pl.pallas_call(
+        functools.partial(
+            interact_kernel, chips=chips, group=group, fields=fields, single=single
+        ),
+        out_shape=made,
         in_specs=[pl.BlockSpec(memory_space=pltpu.SMEM)] + [vmem] * (4 + len(given)),
-        out_specs=[vmem] * len(given),
+        out_specs=[vmem] * len(made),
         scratch_shapes=scratch,
         compiler_params=pltpu.CompilerParams(vmem_limit_bytes=INTERACT_BYTES),
         cost_estimate=pl.CostEstimate(
@@ -413,6 +452,25 @@
         ),
         name="interact",
     )(place, *weights, *given)
+    if single:
+        return list(done), ()
+    blocks = dict(zip(first, done))
+    if second:
+        made = [jax.ShapeDtypeStruct(given[0].shape, BF16)] * len(second)
+        rest = pl.pallas_call(
+            functools.partial(rest_kernel, chips=chips, group=group),
+            out_shape=made,
+            in_specs=[vmem] * len(state),
+            out_specs=[vmem] * len(made),
+            scratch_shapes=[attention],
+            compiler_params=pltpu.CompilerParams(vmem_limit_bytes=INTERACT_BYTES),
+            cost_estimate=pl.CostEstimate(
+                flops=3_000_000_000, bytes_accessed=4_000_000, transcendentals=0
+            ),
+            name="rest",
+        )(*done[len(first) :])
+        blocks.update(zip(second, rest))
+    return [blocks[k] for k in range(chips)], first if second else ()
 
 
 def logit_kernel(w_ref, *refs):
@@ -507,7 +565,7 @@
         return swap(blocks)
 
     weights = (query_weight, key_weight, value_weight, residual_weight)
-    hidden = interact(field_slot, exchange(blocks), chips, weights, fields)
+    hidden, _ = interact(field_slot, exchange(blocks), chips, weights, fields, single)
     sent = exchange(hidden)
 
     slots = jnp.arange(slot_count, dtype=jnp.int32)

time: 71 us -> 70.9 us (level)
  Pallas kernels: 26.9 us -> 28.1 us
  starting transfers between devices: 28.3 us -> 27.1 us
    pallas_call x0 -> x1, Pallas kernels: none -> 2.47 us  [interact(): pl.pallas_call(functools.partial(rest_kernel, chips=chips, group=group),...]
    pallas_call x1, Pallas kernels: 11.3 us -> 10 us  [interact(): pl.pallas_call(functools.partial(interact_kernel, chips=chips, group=grou...]
    ppermute x14, starting transfers between devices: 27.8 us -> 26.6 us  [swap(): out.append(lax.ppermute(blocks[k], 'fld', route))]
where the time goes in v4:
time: 70.9 us; the launch traced here: 70.7 us
  Pallas kernels  28.1 us (40%)
  starting transfers between devices  27.1 us (38%)
  waiting for transfers between devices  13.5 us (19%)
  local copies, waits for them, and re-layouts  0.94 us (1%)
  between operations  0.74 us (1%)
    ppermute x14, starting transfers between devices, swap(): out.append(lax.ppermute(blocks[k], 'fld', route))  26.6 us
    pallas_call x1, Pallas kernels, lookup(): pl.pallas_call(functools.partial(lookup_kernel, step=step, slot_of=slot_o...  13.9 us
    ppermute x14, waiting for transfers between devices, swap(): out.append(lax.ppermute(blocks[k], 'fld', route))  12.1 us
    pallas_call x1, Pallas kernels, interact(): pl.pallas_call(functools.partial(interact_kernel, chips=chips, group=grou...  10 us
    pallas_call x1, Pallas kernels, interact(): pl.pallas_call(functools.partial(rest_kernel, chips=chips, group=group),...  2.47 us
  transfers between devices with their start and end apart: 15, of which 8 were waited for; matrix products, arithmetic and copies ran while one was open for 1% of the time, Pallas kernels for 1%

profile of v4, /device:TPU:0, one launch (start us, length us, event | category | flops | bytes accessed | tf_op | source)
XLA Modules:
  0.0 70.7 jit_solution(15193738237322553293)
XLA Ops:
  0.6 0.0 copy-start
  0.7 0.8 %copy-done.1 = s32[2048,5]{0,1:T(8,128)S(1)} copy-done((s32[2048,5]{0,1:T(8,128)S(1)}, s32[2048,5]{0,1:T(8,128)}, u32[]{:S(2)}) %copy-start.1) | copy-done | bytes 40984
  1.5 13.9 %shard_map.95 = (bf16[8,3,64,128]{3,2,1,0:T(8,128)(2,1)S(1)}, bf16[8,3,64,128]{3,2,1,0:T(8,128)(2,1)S(1)}) custom-call(s32[5,2048]{1,0:T(8,128)S(1)} %bitcast.4, bf16[64,163840]{1,0:T(8,128)(2,1)} %bitcast.6), custom_call_target="tpu_custom_call" | custom-call | flops 35999997952 | bytes 20971520 | tf_op jit(solution)/shard_map/pallas_call | solution.py:138
  15.4 0.5 collective-permute-start
  15.9 1.3 %collective-permute-done.refs_1_ = bf16[8,3,64,128]{3,2,1,0:T(8,128)(2,1)S(1)} collective-permute-done((bf16[8,3,64,128]{3,2,1,0:T(8,128)(2,1)S(1)}, bf16[8,3,64,128]{3,2,1,0:T(8,128)(2,1)S(1)}, u32[]{:S(2)}, u32[]{:S(2)}) %collective-permute-start) | collective-permute-done | bytes 393248 | tf_op jit(solution)/shard_map/ppermute | solution.py:557
  17.3 0.1 pack.1
  17.4 2.9 %collective-permute-start.1 = (bf16[5,64,128]{2,1,0:T(8,128)(2,1)S(1)}, bf16[5,64,128]{2,1,0:T(8,128)(2,1)S(1)}, u32[]{:S(2)}, u32[]{:S(2)}) collective-permute-start(bf16[5,64,128]{2,1,0:T(8,128)(2,1)S(1)} %get-tuple-element.27), channel_id=1, source_target_pairs={{0,2},{2,4},{4,6},{6,8},{8,10},{10,12},{12,14},{14,0},{1,3},{3,5},... | collective-permute-start | bytes 245768 | tf_op jit(solution)/shard_map/ppermute | solution.py:238
  20.3 1.6 %collective-permute-start.2 = (bf16[5,64,128]{2,1,0:T(8,128)(2,1)S(1)}, bf16[5,64,128]{2,1,0:T(8,128)(2,1)S(1)}, u32[]{:S(2)}, u32[]{:S(2)}) collective-permute-start(bf16[5,64,128]{2,1,0:T(8,128)(2,1)S(1)} %get-tuple-element.28), channel_id=1, source_target_pairs={{0,4},{2,6},{4,8},{6,10},{8,12},{10,14},{12,0},{14,2},{1,5},{3,7},... | collective-permute-start | bytes 245768 | tf_op jit(solution)/shard_map/ppermute | solution.py:238
  21.9 2.6 %collective-permute-start.3 = (bf16[5,64,128]{2,1,0:T(8,128)(2,1)S(1)}, bf16[5,64,128]{2,1,0:T(8,128)(2,1)S(1)}, u32[]{:S(2)}, u32[]{:S(2)}) collective-permute-start(bf16[5,64,128]{2,1,0:T(8,128)(2,1)S(1)} %get-tuple-element.29), channel_id=1, source_target_pairs={{0,6},{2,8},{4,10},{6,12},{8,14},{10,0},{12,2},{14,4},{1,7},{3,9},... | collective-permute-start | bytes 245768 | tf_op jit(solution)/shard_map/ppermute | solution.py:238
  24.5 1.2 %collective-permute-start.4 = (bf16[5,64,128]{2,1,0:T(8,128)(2,1)S(1)}, bf16[5,64,128]{2,1,0:T(8,128)(2,1)S(1)}, u32[]{:S(2)}, u32[]{:S(2)}) collective-permute-start(bf16[5,64,128]{2,1,0:T(8,128)(2,1)S(1)} %get-tuple-element.30), channel_id=1, source_target_pairs={{0,8},{2,10},{4,12},{6,14},{8,0},{10,2},{12,4},{14,6},{1,9},{3,11}... | collective-permute-start | bytes 245768 | tf_op jit(solution)/shard_map/ppermute | solution.py:238
  25.7 2.6 %collective-permute-start.5 = (bf16[5,64,128]{2,1,0:T(8,128)(2,1)S(1)}, bf16[5,64,128]{2,1,0:T(8,128)(2,1)S(1)}, u32[]{:S(2)}, u32[]{:S(2)}) collective-permute-start(bf16[5,64,128]{2,1,0:T(8,128)(2,1)S(1)} %get-tuple-element.31), channel_id=1, source_target_pairs={{0,10},{2,12},{4,14},{6,0},{8,2},{10,4},{12,6},{14,8},{1,11},{3,13... | collective-permute-start | bytes 245768 | tf_op jit(solution)/shard_map/ppermute | solution.py:238
  28.3 0.0 collective-permute-done.1.refs_1_
  28.3 1.3 %collective-permute-start.6 = (bf16[5,64,128]{2,1,0:T(8,128)(2,1)S(1)}, bf16[5,64,128]{2,1,0:T(8,128)(2,1)S(1)}, u32[]{:S(2)}, u32[]{:S(2)}) collective-permute-start(bf16[5,64,128]{2,1,0:T(8,128)(2,1)S(1)} %get-tuple-element.32), channel_id=1, source_target_pairs={{0,12},{2,14},{4,0},{6,2},{8,4},{10,6},{12,8},{14,10},{1,13},{3,15... | collective-permute-start | bytes 245768 | tf_op jit(solution)/shard_map/ppermute | solution.py:238
  29.7 1.4 %collective-permute-start.7 = (bf16[5,64,128]{2,1,0:T(8,128)(2,1)S(1)}, bf16[5,64,128]{2,1,0:T(8,128)(2,1)S(1)}, u32[]{:S(2)}, u32[]{:S(2)}) collective-permute-start(bf16[5,64,128]{2,1,0:T(8,128)(2,1)S(1)} %get-tuple-element.33), channel_id=1, source_target_pairs={{0,14},{2,0},{4,2},{6,4},{8,6},{10,8},{12,10},{14,12},{1,15},{3,1}... | collective-permute-start | bytes 245768 | tf_op jit(solution)/shard_map/ppermute | solution.py:238
  31.1 2.2 %collective-permute-done.3.refs_3_ = bf16[5,64,128]{2,1,0:T(8,128)(2,1)S(1)} collective-permute-done((bf16[5,64,128]{2,1,0:T(8,128)(2,1)S(1)}, bf16[5,64,128]{2,1,0:T(8,128)(2,1)S(1)}, u32[]{:S(2)}, u32[]{:S(2)}) %collective-permute-start.3) | collective-permute-done | bytes 81952 | tf_op jit(solution)/shard_map/ppermute | solution.py:238
  33.3 0.7 %collective-permute-done.4.refs_4_ = bf16[5,64,128]{2,1,0:T(8,128)(2,1)S(1)} collective-permute-done((bf16[5,64,128]{2,1,0:T(8,128)(2,1)S(1)}, bf16[5,64,128]{2,1,0:T(8,128)(2,1)S(1)}, u32[]{:S(2)}, u32[]{:S(2)}) %collective-permute-start.4) | collective-permute-done | bytes 81952 | tf_op jit(solution)/shard_map/ppermute | solution.py:238
  34.1 1.9 %collective-permute-done.6.refs_6_ = bf16[5,64,128]{2,1,0:T(8,128)(2,1)S(1)} collective-permute-done((bf16[5,64,128]{2,1,0:T(8,128)(2,1)S(1)}, bf16[5,64,128]{2,1,0:T(8,128)(2,1)S(1)}, u32[]{:S(2)}, u32[]{:S(2)}) %collective-permute-start.6) | collective-permute-done | bytes 81952 | tf_op jit(solution)/shard_map/ppermute | solution.py:238
  36.0 10.0 %interact.1 = (bf16[5,64,128]{2,1,0:T(8,128)(2,1)S(1)}, bf16[5,64,128]{2,1,0:T(8,128)(2,1)S(1)}, bf16[5,64,128]{2,1,0:T(8,128)(2,1)S(1)}, bf16[5,64,128]{2,1,0:T...) custom-call(s32[40]{0:T(128)S(1)} %copy-done.6, ...), custom_call_target="tpu_custom_call" | custom-call | flops 12000000000 | bytes 4000000 | tf_op jit(solution)/shard_map/interact/pallas_call | solution.py:441
  46.1 2.5 %rest.1 = (bf16[5,64,128]{2,1,0:T(8,128)(2,1)S(1)}, bf16[5,64,128]{2,1,0:T(8,128)(2,1)S(1)}, bf16[5,64,128]{2,1,0:T(8,128)(2,1)S(1)}, bf16[5,64,128]{2,1,0:T(8,128)(2,1)S(1)}) custom-call(f32[40,64,128]{2,1,0:T(8,128)S(1)} %get-tuple-element.34.q_s, bf16[32,80,128]{2,1,0:T(8,128)(2,1)S(1)} %get-tuple-element.35.k_s, ...), custom_call_target="tpu_custom_call" | custom-call | flops 3000000000 | bytes 4000000 | tf_op jit(solution)/shard_map/rest/pallas_call | solution.py:460
  48.5 3.8 %collective-permute-start.13 = (bf16[5,64,128]{2,1,0:T(8,128)(2,1)S(1)}, bf16[5,64,128]{2,1,0:T(8,128)(2,1)S(1)}, u32[]{:S(2)}, u32[]{:S(2)}) collective-permute-start(bf16[5,64,128]{2,1,0:T(8,128)(2,1)S(1)} %get-tuple-element.44.refs_6_), channel_id=1, source_target_pairs={{0,12},{2,14},{4,0},{6,2},{8,4},{10,6},{12,8},{14,10},{1,13},{3,15... | collective-permute-start | bytes 245768 | tf_op jit(solution)/shard_map/ppermute | solution.py:238
  52.4 3.3 %collective-permute-start.14 = (bf16[5,64,128]{2,1,0:T(8,128)(2,1)S(1)}, bf16[5,64,128]{2,1,0:T(8,128)(2,1)S(1)}, u32[]{:S(2)}, u32[]{:S(2)}) collective-permute-start(bf16[5,64,128]{2,1,0:T(8,128)(2,1)S(1)} %get-tuple-element.45.refs_7_), channel_id=1, source_target_pairs={{0,14},{2,0},{4,2},{6,4},{8,6},{10,8},{12,10},{14,12},{1,15},{3,1}... | collective-permute-start | bytes 245768 | tf_op jit(solution)/shard_map/ppermute | solution.py:238
  55.7 0.3 fusion
  55.9 0.1 reshape.18.w_ref
  56.0 0.6 collective-permute-start.10
  56.6 4.7 %collective-permute-start.11 = (bf16[5,64,128]{2,1,0:T(8,128)(2,1)S(1)}, bf16[5,64,128]{2,1,0:T(8,128)(2,1)S(1)}, u32[]{:S(2)}, u32[]{:S(2)}) collective-permute-start(bf16[5,64,128]{2,1,0:T(8,128)(2,1)S(1)} %get-tuple-element.42.refs_4_), channel_id=1, source_target_pairs={{0,8},{2,10},{4,12},{6,14},{8,0},{10,2},{12,4},{14,6},{1,9},{3,11}... | collective-permute-start | bytes 245768 | tf_op jit(solution)/shard_map/ppermute | solution.py:238
  61.3 0.5 collective-permute-start.9
  61.8 0.8 %logit.1 = f32[1,128]{1,0:T(1,128)} custom-call(f32[8,320]{1,0:T(8,128)S(1)} %reshape.18.w_ref, bf16[5,64,128]{2,1,0:T(8,128)(2,1)S(1)} %get-tuple-element.38.refs_0_, bf16[5,64,128]{2,1,0:T(8,128)(2,1)S(1)} %get-tuple-element.39.refs_1_, bf16[5,64,128]{2,1,0:T(8,128)(2,1)S(1)} %get-tuple-element.40.refs_2_, ...), custom_call_target="tpu_custom_call" | custom-call | flops 1000000000 | bytes 1000000 | tf_op jit(solution)/shard_map/logit/pallas_call | solution.py:497
  62.5 1.1 %collective-permute-done.8.refs_1_ = bf16[5,64,128]{2,1,0:T(8,128)(2,1)S(1)} collective-permute-done((bf16[5,64,128]{2,1,0:T(8,128)(2,1)S(1)}, bf16[5,64,128]{2,1,0:T(8,128)(2,1)S(1)}, u32[]{:S(2)}, u32[]{:S(2)}) %collective-permute-start.8) | collective-permute-done | bytes 81952 | tf_op jit(solution)/shard_map/ppermute | solution.py:238
  63.6 3.6 %collective-permute-done.10.refs_3_ = bf16[5,64,128]{2,1,0:T(8,128)(2,1)S(1)} collective-permute-done((bf16[5,64,128]{2,1,0:T(8,128)(2,1)S(1)}, bf16[5,64,128]{2,1,0:T(8,128)(2,1)S(1)}, u32[]{:S(2)}, u32[]{:S(2)}) %collective-permute-start.10) | collective-permute-done | bytes 81952 | tf_op jit(solution)/shard_map/ppermute | solution.py:238
  67.2 2.0 %collective-permute-done.11.refs_4_ = bf16[5,64,128]{2,1,0:T(8,128)(2,1)S(1)} collective-permute-done((bf16[5,64,128]{2,1,0:T(8,128)(2,1)S(1)}, bf16[5,64,128]{2,1,0:T(8,128)(2,1)S(1)}, u32[]{:S(2)}, u32[]{:S(2)}) %collective-permute-start.11) | collective-permute-done | bytes 81952 | tf_op jit(solution)/shard_map/ppermute | solution.py:238
  69.3 0.5 collective-permute-done.12.refs_5_
  69.8 0.9 %join.1 = bf16[5,64,1024]{2,1,0:T(8,128)(2,1)} custom-call(bf16[5,64,128]{2,1,0:T(8,128)(2,1)S(1)} %get-tuple-element.38.refs_0_, bf16[5,64,128]{2,1,0:T(8,128)(2,1)S(1)} %collective-permute-done.8.refs_1_, bf16[5,64,128]{2,1,0:T(8,128)(2,1)S(1)} %collective-permute-done.9.refs_2_, bf16[5,64,128]{2,1,0:T(8,128)(2,1)S(1)} %collective-permute-done.10.refs_3_, ...), custom_call_target="tpu_custom_call" | custom-call | tf_op jit(solution)/shard_map/join/pallas_call | solution.py:222
  (21 shorter events, 0.1 us)
Async XLA Ops:
  0.6 55.0 %copy-start = (f32[40,64]{1,0:T(8,128)S(1)}, f32[40,64]{1,0:T(8,128)}, u32[]{:S(2)}) copy-start(f32[40,64]{1,0:T(8,128)} %param.15) | copy-start | bytes 30724
  0.6 0.8 %copy-start.1 = (s32[2048,5]{0,1:T(8,128)S(1)}, s32[2048,5]{0,1:T(8,128)}, u32[]{:S(2)}) copy-start(s32[2048,5]{0,1:T(8,128)} %param.8) | copy-start | bytes 122884
  1.5 34.5 %copy-start.2 = (bf16[2,64,64]{2,1,0:T(8,128)(2,1)S(1)}, bf16[2,64,64]{2,1,0:T(8,128)(2,1)}, u32[]{:S(2)}) copy-start(bf16[2,64,64]{2,1,0:T(8,128)(2,1)} %wq_ref.1) | copy-start | bytes 49156
  1.5 34.5 %copy-start.3 = (bf16[2,64,64]{2,1,0:T(8,128)(2,1)S(1)}, bf16[2,64,64]{2,1,0:T(8,128)(2,1)}, u32[]{:S(2)}) copy-start(bf16[2,64,64]{2,1,0:T(8,128)(2,1)} %wk_ref.1) | copy-start | bytes 49156
  1.5 34.5 %copy-start.4 = (bf16[2,64,64]{2,1,0:T(8,128)(2,1)S(1)}, bf16[2,64,64]{2,1,0:T(8,128)(2,1)}, u32[]{:S(2)}) copy-start(bf16[2,64,64]{2,1,0:T(8,128)(2,1)} %wv_ref.1) | copy-start | bytes 49156
  1.5 34.5 %copy-start.5 = (bf16[2,64,64]{2,1,0:T(8,128)(2,1)S(1)}, bf16[2,64,64]{2,1,0:T(8,128)(2,1)}, u32[]{:S(2)}) copy-start(bf16[2,64,64]{2,1,0:T(8,128)(2,1)} %wr_ref.1) | copy-start | bytes 49156
  1.5 34.5 %copy-start.6 = (s32[40]{0:T(128)S(1)}, s32[40]{0:T(128)}, u32[]{:S(2)}) copy-start(s32[40]{0:T(128)} %place_ref.1) | copy-start | bytes 484
  15.4 1.9 %collective-permute-start = (bf16[8,3,64,128]{3,2,1,0:T(8,128)(2,1)S(1)}, bf16[8,3,64,128]{3,2,1,0:T(8,128)(2,1)S(1)}, u32[]{:S(2)}, u32[]{:S(2)}) collective-permute-start(bf16[8,3,64,128]{3,2,1,0:T(8,128)(2,1)S(1)} %get-tuple-element.25), channel_id=1, source_target_pairs={{0,1},{1,0},{2,3},{3,2},{4,5},{5,4},{6,7},{7,6},{8,9},{9,8},{10,11... | collective-permute-start | bytes 1179656 | tf_op jit(solution)/shard_map/ppermute | solution.py:557
  17.4 10.9 %collective-permute-start.1 = (bf16[5,64,128]{2,1,0:T(8,128)(2,1)S(1)}, bf16[5,64,128]{2,1,0:T(8,128)(2,1)S(1)}, u32[]{:S(2)}, u32[]{:S(2)}) collective-permute-start(bf16[5,64,128]{2,1,0:T(8,128)(2,1)S(1)} %get-tuple-element.27), channel_id=1, source_target_pairs={{0,2},{2,4},{4,6},{6,8},{8,10},{10,12},{12,14},{14,0},{1,3},{3,5},... | collective-permute-start | bytes 245768 | tf_op jit(solution)/shard_map/ppermute | solution.py:238
  20.3 9.3 %collective-permute-start.2 = (bf16[5,64,128]{2,1,0:T(8,128)(2,1)S(1)}, bf16[5,64,128]{2,1,0:T(8,128)(2,1)S(1)}, u32[]{:S(2)}, u32[]{:S(2)}) collective-permute-start(bf16[5,64,128]{2,1,0:T(8,128)(2,1)S(1)} %get-tuple-element.28), channel_id=1, source_target_pairs={{0,4},{2,6},{4,8},{6,10},{8,12},{10,14},{12,0},{14,2},{1,5},{3,7},... | collective-permute-start | bytes 245768 | tf_op jit(solution)/shard_map/ppermute | solution.py:238
  21.9 11.4 %collective-permute-start.3 = (bf16[5,64,128]{2,1,0:T(8,128)(2,1)S(1)}, bf16[5,64,128]{2,1,0:T(8,128)(2,1)S(1)}, u32[]{:S(2)}, u32[]{:S(2)}) collective-permute-start(bf16[5,64,128]{2,1,0:T(8,128)(2,1)S(1)} %get-tuple-element.29), channel_id=1, source_target_pairs={{0,6},{2,8},{4,10},{6,12},{8,14},{10,0},{12,2},{14,4},{1,7},{3,9},... | collective-permute-start | bytes 245768 | tf_op jit(solution)/shard_map/ppermute | solution.py:238
  24.5 9.6 %collective-permute-start.4 = (bf16[5,64,128]{2,1,0:T(8,128)(2,1)S(1)}, bf16[5,64,128]{2,1,0:T(8,128)(2,1)S(1)}, u32[]{:S(2)}, u32[]{:S(2)}) collective-permute-start(bf16[5,64,128]{2,1,0:T(8,128)(2,1)S(1)} %get-tuple-element.30), channel_id=1, source_target_pairs={{0,8},{2,10},{4,12},{6,14},{8,0},{10,2},{12,4},{14,6},{1,9},{3,11}... | collective-permute-start | bytes 245768 | tf_op jit(solution)/shard_map/ppermute | solution.py:238
  25.7 8.4 %collective-permute-start.5 = (bf16[5,64,128]{2,1,0:T(8,128)(2,1)S(1)}, bf16[5,64,128]{2,1,0:T(8,128)(2,1)S(1)}, u32[]{:S(2)}, u32[]{:S(2)}) collective-permute-start(bf16[5,64,128]{2,1,0:T(8,128)(2,1)S(1)} %get-tuple-element.31), channel_id=1, source_target_pairs={{0,10},{2,12},{4,14},{6,0},{8,2},{10,4},{12,6},{14,8},{1,11},{3,13... | collective-permute-start | bytes 245768 | tf_op jit(solution)/shard_map/ppermute | solution.py:238
  28.3 7.7 %collective-permute-start.6 = (bf16[5,64,128]{2,1,0:T(8,128)(2,1)S(1)}, bf16[5,64,128]{2,1,0:T(8,128)(2,1)S(1)}, u32[]{:S(2)}, u32[]{:S(2)}) collective-permute-start(bf16[5,64,128]{2,1,0:T(8,128)(2,1)S(1)} %get-tuple-element.32), channel_id=1, source_target_pairs={{0,12},{2,14},{4,0},{6,2},{8,4},{10,6},{12,8},{14,10},{1,13},{3,15... | collective-permute-start | bytes 245768 | tf_op jit(solution)/shard_map/ppermute | solution.py:238
  29.7 6.3 %collective-permute-start.7 = (bf16[5,64,128]{2,1,0:T(8,128)(2,1)S(1)}, bf16[5,64,128]{2,1,0:T(8,128)(2,1)S(1)}, u32[]{:S(2)}, u32[]{:S(2)}) collective-permute-start(bf16[5,64,128]{2,1,0:T(8,128)(2,1)S(1)} %get-tuple-element.33), channel_id=1, source_target_pairs={{0,14},{2,0},{4,2},{6,4},{8,6},{10,8},{12,10},{14,12},{1,15},{3,1}... | collective-permute-start | bytes 245768 | tf_op jit(solution)/shard_map/ppermute | solution.py:238
  48.5 12.8 %collective-permute-start.13 = (bf16[5,64,128]{2,1,0:T(8,128)(2,1)S(1)}, bf16[5,64,128]{2,1,0:T(8,128)(2,1)S(1)}, u32[]{:S(2)}, u32[]{:S(2)}) collective-permute-start(bf16[5,64,128]{2,1,0:T(8,128)(2,1)S(1)} %get-tuple-element.44.refs_6_), channel_id=1, source_target_pairs={{0,12},{2,14},{4,0},{6,2},{8,4},{10,6},{12,8},{14,10},{1,13},{3,15... | collective-permute-start | bytes 245768 | tf_op jit(solution)/shard_map/ppermute | solution.py:238
  52.4 9.0 %collective-permute-start.14 = (bf16[5,64,128]{2,1,0:T(8,128)(2,1)S(1)}, bf16[5,64,128]{2,1,0:T(8,128)(2,1)S(1)}, u32[]{:S(2)}, u32[]{:S(2)}) collective-permute-start(bf16[5,64,128]{2,1,0:T(8,128)(2,1)S(1)} %get-tuple-element.45.refs_7_), channel_id=1, source_target_pairs={{0,14},{2,0},{4,2},{6,4},{8,6},{10,8},{12,10},{14,12},{1,15},{3,1}... | collective-permute-start | bytes 245768 | tf_op jit(solution)/shard_map/ppermute | solution.py:238
  56.0 7.6 %collective-permute-start.8 = (bf16[5,64,128]{2,1,0:T(8,128)(2,1)S(1)}, bf16[5,64,128]{2,1,0:T(8,128)(2,1)S(1)}, u32[]{:S(2)}, u32[]{:S(2)}) collective-permute-start(bf16[5,64,128]{2,1,0:T(8,128)(2,1)S(1)} %get-tuple-element.39.refs_1_), channel_id=1, source_target_pairs={{0,2},{2,4},{4,6},{6,8},{8,10},{10,12},{12,14},{14,0},{1,3},{3,5},... | collective-permute-start | bytes 245768 | tf_op jit(solution)/shard_map/ppermute | solution.py:238
  56.0 11.2 %collective-permute-start.10 = (bf16[5,64,128]{2,1,0:T(8,128)(2,1)S(1)}, bf16[5,64,128]{2,1,0:T(8,128)(2,1)S(1)}, u32[]{:S(2)}, u32[]{:S(2)}) collective-permute-start(bf16[5,64,128]{2,1,0:T(8,128)(2,1)S(1)} %get-tuple-element.41.refs_3_), channel_id=1, source_target_pairs={{0,6},{2,8},{4,10},{6,12},{8,14},{10,0},{12,2},{14,4},{1,7},{3,9},... | collective-permute-start | bytes 245768 | tf_op jit(solution)/shard_map/ppermute | solution.py:238
  56.6 12.7 %collective-permute-start.11 = (bf16[5,64,128]{2,1,0:T(8,128)(2,1)S(1)}, bf16[5,64,128]{2,1,0:T(8,128)(2,1)S(1)}, u32[]{:S(2)}, u32[]{:S(2)}) collective-permute-start(bf16[5,64,128]{2,1,0:T(8,128)(2,1)S(1)} %get-tuple-element.42.refs_4_), channel_id=1, source_target_pairs={{0,8},{2,10},{4,12},{6,14},{8,0},{10,2},{12,4},{14,6},{1,9},{3,11}... | collective-permute-start | bytes 245768 | tf_op jit(solution)/shard_map/ppermute | solution.py:238
  61.3 8.5 %collective-permute-start.12 = (bf16[5,64,128]{2,1,0:T(8,128)(2,1)S(1)}, bf16[5,64,128]{2,1,0:T(8,128)(2,1)S(1)}, u32[]{:S(2)}, u32[]{:S(2)}) collective-permute-start(bf16[5,64,128]{2,1,0:T(8,128)(2,1)S(1)} %get-tuple-element.43.refs_5_), channel_id=1, source_target_pairs={{0,10},{2,12},{4,14},{6,0},{8,2},{10,4},{12,6},{14,8},{1,11},{3,13... | collective-permute-start | bytes 245768 | tf_op jit(solution)/shard_map/ppermute | solution.py:238
  61.3 8.5 %collective-permute-start.9 = (bf16[5,64,128]{2,1,0:T(8,128)(2,1)S(1)}, bf16[5,64,128]{2,1,0:T(8,128)(2,1)S(1)}, u32[]{:S(2)}, u32[]{:S(2)}) collective-permute-start(bf16[5,64,128]{2,1,0:T(8,128)(2,1)S(1)} %get-tuple-element.40.refs_2_), channel_id=1, source_target_pairs={{0,4},{2,6},{4,8},{6,10},{8,12},{10,14},{12,0},{14,2},{1,5},{3,7},... | collective-permute-start | bytes 245768 | tf_op jit(solution)/shard_map/ppermute | solution.py:238

commit v5 on v3

--- a/solution.py
+++ b/solution.py
@@ -75,7 +75,6 @@
             odd_ref[pl.ds(j * blocks + b, 1), :] = (rows >> 7) & 1
     rows_copy = pltpu.make_async_copy(lines, row_ref, row_sem)
     rows_copy.start()
-    rows_copy.wait()
     for j in range(slots):
 
         def chunk(c, carry):
@@ -100,6 +99,8 @@
             return carry
 
         lax.fori_loop(bounds[j], bounds[j + 1], chunk, 0)
+        if j == 0:
+            rows_copy.wait()
 
         def some_blocks(i, carry, j=j, out_ref=None, ahead=0):
             def some(n, carry):
@@ -128,7 +129,7 @@
     buffers = min(4, owned // step)
     reps = len(bounds_of[0])
     blocks = chips * reps
-    batch = divisor(chips, (4, 2, 1))
+    batch = divisor(chips, (8, 4, 2, 1))
     vmem = pl.BlockSpec(memory_space=pltpu.VMEM)
     anywhere = pl.BlockSpec(memory_space=pl.ANY)
     return pl.pallas_call(
@@ -254,7 +255,7 @@
             v_s[i, 2 * ROWS * t : 2 * ROWS * (t + 1)] = two.astype(BF16)
         return carry
 
-    lax.fori_loop(0, fields // 2, pair, 0, unroll=divisor(fields // 2, (10, 8, 5, 4, 2, 1)))
+    lax.fori_loop(0, fields // 2, pair, 0, unroll=divisor(fields // 2, (20, 10, 8, 5, 4, 2, 1)))
 
     def turn(i, carry):
         rows = [
@@ -388,7 +389,7 @@
 
 def interact(place, given, chips, weights, fields):
     per, width, lanes = given[0].shape[-3:]
-    group = divisor(math.gcd(fields, chips), (4, 2, 1))
+    group = divisor(math.gcd(fields, chips), (8, 4, 2, 1))
     wide = pltpu.VMEM((fields, width, lanes), F32)
     vmem = pl.BlockSpec(memory_space=pltpu.VMEM)
     scratch = [

time: 71 us -> 70.3 us (level)
  no operation moved by 1% of the time
where the time goes in v5:
time: 70.3 us; the launch traced here: 70.1 us
  starting transfers between devices  28.3 us (40%)
  Pallas kernels  26.2 us (37%)
  waiting for transfers between devices  13.6 us (19%)
  local copies, waits for them, and re-layouts  0.94 us (1%)
  between operations  0.73 us (1%)
    ppermute x14, starting transfers between devices, swap(): lax.ppermute(blocks[k], 'fld', [(i, (i + k) % chips) for i in range(chips)])  27.8 us
    pallas_call x1, Pallas kernels, lookup(): pl.pallas_call(functools.partial(lookup_kernel, step=step, slot_of=slot_o...  13.5 us
    ppermute x14, waiting for transfers between devices, swap(): lax.ppermute(blocks[k], 'fld', [(i, (i + k) % chips) for i in range(chips)])  12.3 us
    pallas_call x1, Pallas kernels, interact(): pl.pallas_call(functools.partial(interact_kernel, chips=chips, group=grou...  10.9 us
  transfers between devices with their start and end apart: 15, of which 8 were waited for; matrix products, arithmetic and copies ran while one was open for 1% of the time, Pallas kernels for 1%

profile of v5, /device:TPU:0, one launch (start us, length us, event | category | flops | bytes accessed | tf_op | source)
XLA Modules:
  0.0 70.1 jit_solution(1123230612358516395)
XLA Ops:
  0.6 0.0 copy-start
  0.7 0.8 %copy-done.1 = s32[2048,5]{0,1:T(8,128)S(1)} copy-done((s32[2048,5]{0,1:T(8,128)S(1)}, s32[2048,5]{0,1:T(8,128)}, u32[]{:S(2)}) %copy-start.1) | copy-done | bytes 40984
  1.5 13.5 %shard_map.95 = (bf16[8,3,64,128]{3,2,1,0:T(8,128)(2,1)S(1)}, bf16[8,3,64,128]{3,2,1,0:T(8,128)(2,1)S(1)}) custom-call(s32[5,2048]{1,0:T(8,128)S(1)} %bitcast.4, bf16[64,163840]{1,0:T(8,128)(2,1)} %bitcast.6), custom_call_target="tpu_custom_call" | custom-call | flops 35999997952 | bytes 20971520 | tf_op jit(solution)/shard_map/pallas_call | solution.py:135
  15.0 0.5 collective-permute-start
  15.5 1.3 %collective-permute-done.refs_1_ = bf16[8,3,64,128]{3,2,1,0:T(8,128)(2,1)S(1)} collective-permute-done((bf16[8,3,64,128]{3,2,1,0:T(8,128)(2,1)S(1)}, bf16[8,3,64,128]{3,2,1,0:T(8,128)(2,1)S(1)}, u32[]{:S(2)}, u32[]{:S(2)}) %collective-permute-start) | collective-permute-done | bytes 393248 | tf_op jit(solution)/shard_map/ppermute | solution.py:500
  16.9 0.1 pack.1
  17.0 3.0 %collective-permute-start.1 = (bf16[5,64,128]{2,1,0:T(8,128)(2,1)S(1)}, bf16[5,64,128]{2,1,0:T(8,128)(2,1)S(1)}, u32[]{:S(2)}, u32[]{:S(2)}) collective-permute-start(bf16[5,64,128]{2,1,0:T(8,128)(2,1)S(1)} %get-tuple-element.23), channel_id=1, source_target_pairs={{0,2},{2,4},{4,6},{6,8},{8,10},{10,12},{12,14},{14,0},{1,3},{3,5},... | collective-permute-start | bytes 245768 | tf_op jit(solution)/shard_map/ppermute | solution.py:232
  20.0 1.6 %collective-permute-start.2 = (bf16[5,64,128]{2,1,0:T(8,128)(2,1)S(1)}, bf16[5,64,128]{2,1,0:T(8,128)(2,1)S(1)}, u32[]{:S(2)}, u32[]{:S(2)}) collective-permute-start(bf16[5,64,128]{2,1,0:T(8,128)(2,1)S(1)} %get-tuple-element.24), channel_id=1, source_target_pairs={{0,4},{2,6},{4,8},{6,10},{8,12},{10,14},{12,0},{14,2},{1,5},{3,7},... | collective-permute-start | bytes 245768 | tf_op jit(solution)/shard_map/ppermute | solution.py:232
  21.6 2.6 %collective-permute-start.3 = (bf16[5,64,128]{2,1,0:T(8,128)(2,1)S(1)}, bf16[5,64,128]{2,1,0:T(8,128)(2,1)S(1)}, u32[]{:S(2)}, u32[]{:S(2)}) collective-permute-start(bf16[5,64,128]{2,1,0:T(8,128)(2,1)S(1)} %get-tuple-element.25), channel_id=1, source_target_pairs={{0,6},{2,8},{4,10},{6,12},{8,14},{10,0},{12,2},{14,4},{1,7},{3,9},... | collective-permute-start | bytes 245768 | tf_op jit(solution)/shard_map/ppermute | solution.py:232
  24.1 1.2 %collective-permute-start.4 = (bf16[5,64,128]{2,1,0:T(8,128)(2,1)S(1)}, bf16[5,64,128]{2,1,0:T(8,128)(2,1)S(1)}, u32[]{:S(2)}, u32[]{:S(2)}) collective-permute-start(bf16[5,64,128]{2,1,0:T(8,128)(2,1)S(1)} %get-tuple-element.26), channel_id=1, source_target_pairs={{0,8},{2,10},{4,12},{6,14},{8,0},{10,2},{12,4},{14,6},{1,9},{3,11}... | collective-permute-start | bytes 245768 | tf_op jit(solution)/shard_map/ppermute | solution.py:232
  25.4 2.6 %collective-permute-start.5 = (bf16[5,64,128]{2,1,0:T(8,128)(2,1)S(1)}, bf16[5,64,128]{2,1,0:T(8,128)(2,1)S(1)}, u32[]{:S(2)}, u32[]{:S(2)}) collective-permute-start(bf16[5,64,128]{2,1,0:T(8,128)(2,1)S(1)} %get-tuple-element.27), channel_id=1, source_target_pairs={{0,10},{2,12},{4,14},{6,0},{8,2},{10,4},{12,6},{14,8},{1,11},{3,13... | collective-permute-start | bytes 245768 | tf_op jit(solution)/shard_map/ppermute | solution.py:232
  28.0 1.3 %collective-permute-start.6 = (bf16[5,64,128]{2,1,0:T(8,128)(2,1)S(1)}, bf16[5,64,128]{2,1,0:T(8,128)(2,1)S(1)}, u32[]{:S(2)}, u32[]{:S(2)}) collective-permute-start(bf16[5,64,128]{2,1,0:T(8,128)(2,1)S(1)} %get-tuple-element.28), channel_id=1, source_target_pairs={{0,12},{2,14},{4,0},{6,2},{8,4},{10,6},{12,8},{14,10},{1,13},{3,15... | collective-permute-start | bytes 245768 | tf_op jit(solution)/shard_map/ppermute | solution.py:232
  29.3 0.0 collective-permute-done.2.refs_2_
  29.3 1.4 %collective-permute-start.7 = (bf16[5,64,128]{2,1,0:T(8,128)(2,1)S(1)}, bf16[5,64,128]{2,1,0:T(8,128)(2,1)S(1)}, u32[]{:S(2)}, u32[]{:S(2)}) collective-permute-start(bf16[5,64,128]{2,1,0:T(8,128)(2,1)S(1)} %get-tuple-element.29), channel_id=1, source_target_pairs={{0,14},{2,0},{4,2},{6,4},{8,6},{10,8},{12,10},{14,12},{1,15},{3,1}... | collective-permute-start | bytes 245768 | tf_op jit(solution)/shard_map/ppermute | solution.py:232
  30.8 2.2 %collective-permute-done.3.refs_3_ = bf16[5,64,128]{2,1,0:T(8,128)(2,1)S(1)} collective-permute-done((bf16[5,64,128]{2,1,0:T(8,128)(2,1)S(1)}, bf16[5,64,128]{2,1,0:T(8,128)(2,1)S(1)}, u32[]{:S(2)}, u32[]{:S(2)}) %collective-permute-start.3) | collective-permute-done | bytes 81952 | tf_op jit(solution)/shard_map/ppermute | solution.py:232
  33.0 0.7 %collective-permute-done.4.refs_4_ = bf16[5,64,128]{2,1,0:T(8,128)(2,1)S(1)} collective-permute-done((bf16[5,64,128]{2,1,0:T(8,128)(2,1)S(1)}, bf16[5,64,128]{2,1,0:T(8,128)(2,1)S(1)}, u32[]{:S(2)}, u32[]{:S(2)}) %collective-permute-start.4) | collective-permute-done | bytes 81952 | tf_op jit(solution)/shard_map/ppermute | solution.py:232
  33.7 1.9 %collective-permute-done.6.refs_6_ = bf16[5,64,128]{2,1,0:T(8,128)(2,1)S(1)} collective-permute-done((bf16[5,64,128]{2,1,0:T(8,128)(2,1)S(1)}, bf16[5,64,128]{2,1,0:T(8,128)(2,1)S(1)}, u32[]{:S(2)}, u32[]{:S(2)}) %collective-permute-start.6) | collective-permute-done | bytes 81952 | tf_op jit(solution)/shard_map/ppermute | solution.py:232
  35.7 10.9 %interact.1 = (bf16[5,64,128]{2,1,0:T(8,128)(2,1)S(1)}, bf16[5,64,128]{2,1,0:T(8,128)(2,1)S(1)}, bf16[5,64,128]{2,1,0:T(8,128)(2,1)S(1)}, bf16[5,64,128]{2,1,0:T...) custom-call(s32[40]{0:T(128)S(1)} %copy-done.6, ...), custom_call_target="tpu_custom_call" | custom-call | flops 12000000000 | bytes 4000000 | tf_op jit(solution)/shard_map/interact/pallas_call | solution.py:405
  46.6 4.7 %collective-permute-start.10 = (bf16[5,64,128]{2,1,0:T(8,128)(2,1)S(1)}, bf16[5,64,128]{2,1,0:T(8,128)(2,1)S(1)}, u32[]{:S(2)}, u32[]{:S(2)}) collective-permute-start(bf16[5,64,128]{2,1,0:T(8,128)(2,1)S(1)} %get-tuple-element.33.refs_3_), channel_id=1, source_target_pairs={{0,6},{2,8},{4,10},{6,12},{8,14},{10,0},{12,2},{14,4},{1,7},{3,9},... | collective-permute-start | bytes 245768 | tf_op jit(solution)/shard_map/ppermute | solution.py:232
  51.3 1.3 %collective-permute-start.11 = (bf16[5,64,128]{2,1,0:T(8,128)(2,1)S(1)}, bf16[5,64,128]{2,1,0:T(8,128)(2,1)S(1)}, u32[]{:S(2)}, u32[]{:S(2)}) collective-permute-start(bf16[5,64,128]{2,1,0:T(8,128)(2,1)S(1)} %get-tuple-element.34.refs_4_), channel_id=1, source_target_pairs={{0,8},{2,10},{4,12},{6,14},{8,0},{10,2},{12,4},{14,6},{1,9},{3,11}... | collective-permute-start | bytes 245768 | tf_op jit(solution)/shard_map/ppermute | solution.py:232
  52.6 0.3 fusion
  52.9 0.1 reshape.18.w_ref
  53.0 1.1 %collective-permute-start.12 = (bf16[5,64,128]{2,1,0:T(8,128)(2,1)S(1)}, bf16[5,64,128]{2,1,0:T(8,128)(2,1)S(1)}, u32[]{:S(2)}, u32[]{:S(2)}) collective-permute-start(bf16[5,64,128]{2,1,0:T(8,128)(2,1)S(1)} %get-tuple-element.35.refs_5_), channel_id=1, source_target_pairs={{0,10},{2,12},{4,14},{6,0},{8,2},{10,4},{12,6},{14,8},{1,11},{3,13... | collective-permute-start | bytes 245768 | tf_op jit(solution)/shard_map/ppermute | solution.py:232
  54.0 1.5 %collective-permute-start.13 = (bf16[5,64,128]{2,1,0:T(8,128)(2,1)S(1)}, bf16[5,64,128]{2,1,0:T(8,128)(2,1)S(1)}, u32[]{:S(2)}, u32[]{:S(2)}) collective-permute-start(bf16[5,64,128]{2,1,0:T(8,128)(2,1)S(1)} %get-tuple-element.36.refs_6_), channel_id=1, source_target_pairs={{0,12},{2,14},{4,0},{6,2},{8,4},{10,6},{12,8},{14,10},{1,13},{3,15... | collective-permute-start | bytes 245768 | tf_op jit(solution)/shard_map/ppermute | solution.py:232
  55.5 1.4 %collective-permute-start.14 = (bf16[5,64,128]{2,1,0:T(8,128)(2,1)S(1)}, bf16[5,64,128]{2,1,0:T(8,128)(2,1)S(1)}, u32[]{:S(2)}, u32[]{:S(2)}) collective-permute-start(bf16[5,64,128]{2,1,0:T(8,128)(2,1)S(1)} %get-tuple-element.37.refs_7_), channel_id=1, source_target_pairs={{0,14},{2,0},{4,2},{6,4},{8,6},{10,8},{12,10},{14,12},{1,15},{3,1}... | collective-permute-start | bytes 245768 | tf_op jit(solution)/shard_map/ppermute | solution.py:232
  57.0 1.2 %collective-permute-done.10.refs_3_ = bf16[5,64,128]{2,1,0:T(8,128)(2,1)S(1)} collective-permute-done((bf16[5,64,128]{2,1,0:T(8,128)(2,1)S(1)}, bf16[5,64,128]{2,1,0:T(8,128)(2,1)S(1)}, u32[]{:S(2)}, u32[]{:S(2)}) %collective-permute-start.10) | collective-permute-done | bytes 81952 | tf_op jit(solution)/shard_map/ppermute | solution.py:232
  58.2 1.8 %collective-permute-done.11.refs_4_ = bf16[5,64,128]{2,1,0:T(8,128)(2,1)S(1)} collective-permute-done((bf16[5,64,128]{2,1,0:T(8,128)(2,1)S(1)}, bf16[5,64,128]{2,1,0:T(8,128)(2,1)S(1)}, u32[]{:S(2)}, u32[]{:S(2)}) %collective-permute-start.11) | collective-permute-done | bytes 81952 | tf_op jit(solution)/shard_map/ppermute | solution.py:232
  59.9 4.0 %collective-permute-start.9 = (bf16[5,64,128]{2,1,0:T(8,128)(2,1)S(1)}, bf16[5,64,128]{2,1,0:T(8,128)(2,1)S(1)}, u32[]{:S(2)}, u32[]{:S(2)}) collective-permute-start(bf16[5,64,128]{2,1,0:T(8,128)(2,1)S(1)} %get-tuple-element.32.refs_2_), channel_id=1, source_target_pairs={{0,4},{2,6},{4,8},{6,10},{8,12},{10,14},{12,0},{14,2},{1,5},{3,7},... | collective-permute-start | bytes 245768 | tf_op jit(solution)/shard_map/ppermute | solution.py:232
  64.0 0.7 %logit.1 = f32[1,128]{1,0:T(1,128)} custom-call(f32[8,320]{1,0:T(8,128)S(1)} %reshape.18.w_ref, bf16[5,64,128]{2,1,0:T(8,128)(2,1)S(1)} %get-tuple-element.30.refs_0_, bf16[5,64,128]{2,1,0:T(8,128)(2,1)S(1)} %get-tuple-element.31.refs_1_, bf16[5,64,128]{2,1,0:T(8,128)(2,1)S(1)} %get-tuple-element.32.refs_2_, ...), custom_call_target="tpu_custom_call" | custom-call | flops 1000000000 | bytes 1000000 | tf_op jit(solution)/shard_map/logit/pallas_call | solution.py:440
  64.7 0.6 collective-permute-done.8.refs_1_
  65.3 3.9 %collective-permute-done.9.refs_2_ = bf16[5,64,128]{2,1,0:T(8,128)(2,1)S(1)} collective-permute-done((bf16[5,64,128]{2,1,0:T(8,128)(2,1)S(1)}, bf16[5,64,128]{2,1,0:T(8,128)(2,1)S(1)}, u32[]{:S(2)}, u32[]{:S(2)}) %collective-permute-start.9) | collective-permute-done | bytes 81952 | tf_op jit(solution)/shard_map/ppermute | solution.py:232
  69.2 0.9 %join.1 = bf16[5,64,1024]{2,1,0:T(8,128)(2,1)} custom-call(bf16[5,64,128]{2,1,0:T(8,128)(2,1)S(1)} %get-tuple-element.30.refs_0_, bf16[5,64,128]{2,1,0:T(8,128)(2,1)S(1)} %collective-permute-done.8.refs_1_, bf16[5,64,128]{2,1,0:T(8,128)(2,1)S(1)} %collective-permute-done.9.refs_2_, bf16[5,64,128]{2,1,0:T(8,128)(2,1)S(1)} %collective-permute-done.10.refs_3_, ...), custom_call_target="tpu_custom_call" | custom-call | tf_op jit(solution)/shard_map/join/pallas_call | solution.py:217
  (20 shorter events, 0.1 us)
Async XLA Ops:
  0.6 52.0 %copy-start = (f32[40,64]{1,0:T(8,128)S(1)}, f32[40,64]{1,0:T(8,128)}, u32[]{:S(2)}) copy-start(f32[40,64]{1,0:T(8,128)} %param.15) | copy-start | bytes 30724
  0.6 0.8 %copy-start.1 = (s32[2048,5]{0,1:T(8,128)S(1)}, s32[2048,5]{0,1:T(8,128)}, u32[]{:S(2)}) copy-start(s32[2048,5]{0,1:T(8,128)} %param.8) | copy-start | bytes 122884
  1.5 34.1 %copy-start.2 = (bf16[2,64,64]{2,1,0:T(8,128)(2,1)S(1)}, bf16[2,64,64]{2,1,0:T(8,128)(2,1)}, u32[]{:S(2)}) copy-start(bf16[2,64,64]{2,1,0:T(8,128)(2,1)} %wq_ref.1) | copy-start | bytes 49156
  1.5 34.1 %copy-start.3 = (bf16[2,64,64]{2,1,0:T(8,128)(2,1)S(1)}, bf16[2,64,64]{2,1,0:T(8,128)(2,1)}, u32[]{:S(2)}) copy-start(bf16[2,64,64]{2,1,0:T(8,128)(2,1)} %wk_ref.1) | copy-start | bytes 49156
  1.5 34.1 %copy-start.4 = (bf16[2,64,64]{2,1,0:T(8,128)(2,1)S(1)}, bf16[2,64,64]{2,1,0:T(8,128)(2,1)}, u32[]{:S(2)}) copy-start(bf16[2,64,64]{2,1,0:T(8,128)(2,1)} %wv_ref.1) | copy-start | bytes 49156
  1.5 34.1 %copy-start.5 = (bf16[2,64,64]{2,1,0:T(8,128)(2,1)S(1)}, bf16[2,64,64]{2,1,0:T(8,128)(2,1)}, u32[]{:S(2)}) copy-start(bf16[2,64,64]{2,1,0:T(8,128)(2,1)} %wr_ref.1) | copy-start | bytes 49156
  1.5 34.2 %copy-start.6 = (s32[40]{0:T(128)S(1)}, s32[40]{0:T(128)}, u32[]{:S(2)}) copy-start(s32[40]{0:T(128)} %place_ref.1) | copy-start | bytes 484
  15.0 1.9 %collective-permute-start = (bf16[8,3,64,128]{3,2,1,0:T(8,128)(2,1)S(1)}, bf16[8,3,64,128]{3,2,1,0:T(8,128)(2,1)S(1)}, u32[]{:S(2)}, u32[]{:S(2)}) collective-permute-start(bf16[8,3,64,128]{3,2,1,0:T(8,128)(2,1)S(1)} %get-tuple-element.21), channel_id=1, source_target_pairs={{0,1},{1,0},{2,3},{3,2},{4,5},{5,4},{6,7},{7,6},{8,9},{9,8},{10,11... | collective-permute-start | bytes 1179656 | tf_op jit(solution)/shard_map/ppermute | solution.py:500
  17.0 11.0 %collective-permute-start.1 = (bf16[5,64,128]{2,1,0:T(8,128)(2,1)S(1)}, bf16[5,64,128]{2,1,0:T(8,128)(2,1)S(1)}, u32[]{:S(2)}, u32[]{:S(2)}) collective-permute-start(bf16[5,64,128]{2,1,0:T(8,128)(2,1)S(1)} %get-tuple-element.23), channel_id=1, source_target_pairs={{0,2},{2,4},{4,6},{6,8},{8,10},{10,12},{12,14},{14,0},{1,3},{3,5},... | collective-permute-start | bytes 245768 | tf_op jit(solution)/shard_map/ppermute | solution.py:232
  20.0 9.3 %collective-permute-start.2 = (bf16[5,64,128]{2,1,0:T(8,128)(2,1)S(1)}, bf16[5,64,128]{2,1,0:T(8,128)(2,1)S(1)}, u32[]{:S(2)}, u32[]{:S(2)}) collective-permute-start(bf16[5,64,128]{2,1,0:T(8,128)(2,1)S(1)} %get-tuple-element.24), channel_id=1, source_target_pairs={{0,4},{2,6},{4,8},{6,10},{8,12},{10,14},{12,0},{14,2},{1,5},{3,7},... | collective-permute-start | bytes 245768 | tf_op jit(solution)/shard_map/ppermute | solution.py:232
  21.6 11.4 %collective-permute-start.3 = (bf16[5,64,128]{2,1,0:T(8,128)(2,1)S(1)}, bf16[5,64,128]{2,1,0:T(8,128)(2,1)S(1)}, u32[]{:S(2)}, u32[]{:S(2)}) collective-permute-start(bf16[5,64,128]{2,1,0:T(8,128)(2,1)S(1)} %get-tuple-element.25), channel_id=1, source_target_pairs={{0,6},{2,8},{4,10},{6,12},{8,14},{10,0},{12,2},{14,4},{1,7},{3,9},... | collective-permute-start | bytes 245768 | tf_op jit(solution)/shard_map/ppermute | solution.py:232
  24.1 9.6 %collective-permute-start.4 = (bf16[5,64,128]{2,1,0:T(8,128)(2,1)S(1)}, bf16[5,64,128]{2,1,0:T(8,128)(2,1)S(1)}, u32[]{:S(2)}, u32[]{:S(2)}) collective-permute-start(bf16[5,64,128]{2,1,0:T(8,128)(2,1)S(1)} %get-tuple-element.26), channel_id=1, source_target_pairs={{0,8},{2,10},{4,12},{6,14},{8,0},{10,2},{12,4},{14,6},{1,9},{3,11}... | collective-permute-start | bytes 245768 | tf_op jit(solution)/shard_map/ppermute | solution.py:232
  25.4 8.4 %collective-permute-start.5 = (bf16[5,64,128]{2,1,0:T(8,128)(2,1)S(1)}, bf16[5,64,128]{2,1,0:T(8,128)(2,1)S(1)}, u32[]{:S(2)}, u32[]{:S(2)}) collective-permute-start(bf16[5,64,128]{2,1,0:T(8,128)(2,1)S(1)} %get-tuple-element.27), channel_id=1, source_target_pairs={{0,10},{2,12},{4,14},{6,0},{8,2},{10,4},{12,6},{14,8},{1,11},{3,13... | collective-permute-start | bytes 245768 | tf_op jit(solution)/shard_map/ppermute | solution.py:232
  28.0 7.7 %collective-permute-start.6 = (bf16[5,64,128]{2,1,0:T(8,128)(2,1)S(1)}, bf16[5,64,128]{2,1,0:T(8,128)(2,1)S(1)}, u32[]{:S(2)}, u32[]{:S(2)}) collective-permute-start(bf16[5,64,128]{2,1,0:T(8,128)(2,1)S(1)} %get-tuple-element.28), channel_id=1, source_target_pairs={{0,12},{2,14},{4,0},{6,2},{8,4},{10,6},{12,8},{14,10},{1,13},{3,15... | collective-permute-start | bytes 245768 | tf_op jit(solution)/shard_map/ppermute | solution.py:232
  29.3 6.3 %collective-permute-start.7 = (bf16[5,64,128]{2,1,0:T(8,128)(2,1)S(1)}, bf16[5,64,128]{2,1,0:T(8,128)(2,1)S(1)}, u32[]{:S(2)}, u32[]{:S(2)}) collective-permute-start(bf16[5,64,128]{2,1,0:T(8,128)(2,1)S(1)} %get-tuple-element.29), channel_id=1, source_target_pairs={{0,14},{2,0},{4,2},{6,4},{8,6},{10,8},{12,10},{14,12},{1,15},{3,1}... | collective-permute-start | bytes 245768 | tf_op jit(solution)/shard_map/ppermute | solution.py:232
  46.6 11.6 %collective-permute-start.10 = (bf16[5,64,128]{2,1,0:T(8,128)(2,1)S(1)}, bf16[5,64,128]{2,1,0:T(8,128)(2,1)S(1)}, u32[]{:S(2)}, u32[]{:S(2)}) collective-permute-start(bf16[5,64,128]{2,1,0:T(8,128)(2,1)S(1)} %get-tuple-element.33.refs_3_), channel_id=1, source_target_pairs={{0,6},{2,8},{4,10},{6,12},{8,14},{10,0},{12,2},{14,4},{1,7},{3,9},... | collective-permute-start | bytes 245768 | tf_op jit(solution)/shard_map/ppermute | solution.py:232
  51.3 8.6 %collective-permute-start.11 = (bf16[5,64,128]{2,1,0:T(8,128)(2,1)S(1)}, bf16[5,64,128]{2,1,0:T(8,128)(2,1)S(1)}, u32[]{:S(2)}, u32[]{:S(2)}) collective-permute-start(bf16[5,64,128]{2,1,0:T(8,128)(2,1)S(1)} %get-tuple-element.34.refs_4_), channel_id=1, source_target_pairs={{0,8},{2,10},{4,12},{6,14},{8,0},{10,2},{12,4},{14,6},{1,9},{3,11}... | collective-permute-start | bytes 245768 | tf_op jit(solution)/shard_map/ppermute | solution.py:232
  53.0 11.7 %collective-permute-start.12 = (bf16[5,64,128]{2,1,0:T(8,128)(2,1)S(1)}, bf16[5,64,128]{2,1,0:T(8,128)(2,1)S(1)}, u32[]{:S(2)}, u32[]{:S(2)}) collective-permute-start(bf16[5,64,128]{2,1,0:T(8,128)(2,1)S(1)} %get-tuple-element.35.refs_5_), channel_id=1, source_target_pairs={{0,10},{2,12},{4,14},{6,0},{8,2},{10,4},{12,6},{14,8},{1,11},{3,13... | collective-permute-start | bytes 245768 | tf_op jit(solution)/shard_map/ppermute | solution.py:232
  54.0 10.7 %collective-permute-start.13 = (bf16[5,64,128]{2,1,0:T(8,128)(2,1)S(1)}, bf16[5,64,128]{2,1,0:T(8,128)(2,1)S(1)}, u32[]{:S(2)}, u32[]{:S(2)}) collective-permute-start(bf16[5,64,128]{2,1,0:T(8,128)(2,1)S(1)} %get-tuple-element.36.refs_6_), channel_id=1, source_target_pairs={{0,12},{2,14},{4,0},{6,2},{8,4},{10,6},{12,8},{14,10},{1,13},{3,15... | collective-permute-start | bytes 245768 | tf_op jit(solution)/shard_map/ppermute | solution.py:232
  55.5 9.2 %collective-permute-start.14 = (bf16[5,64,128]{2,1,0:T(8,128)(2,1)S(1)}, bf16[5,64,128]{2,1,0:T(8,128)(2,1)S(1)}, u32[]{:S(2)}, u32[]{:S(2)}) collective-permute-start(bf16[5,64,128]{2,1,0:T(8,128)(2,1)S(1)} %get-tuple-element.37.refs_7_), channel_id=1, source_target_pairs={{0,14},{2,0},{4,2},{6,4},{8,6},{10,8},{12,10},{14,12},{1,15},{3,1}... | collective-permute-start | bytes 245768 | tf_op jit(solution)/shard_map/ppermute | solution.py:232
  58.2 7.1 %collective-permute-start.8 = (bf16[5,64,128]{2,1,0:T(8,128)(2,1)S(1)}, bf16[5,64,128]{2,1,0:T(8,128)(2,1)S(1)}, u32[]{:S(2)}, u32[]{:S(2)}) collective-permute-start(bf16[5,64,128]{2,1,0:T(8,128)(2,1)S(1)} %get-tuple-element.31.refs_1_), channel_id=1, source_target_pairs={{0,2},{2,4},{4,6},{6,8},{8,10},{10,12},{12,14},{14,0},{1,3},{3,5},... | collective-permute-start | bytes 245768 | tf_op jit(solution)/shard_map/ppermute | solution.py:232
  59.9 9.3 %collective-permute-start.9 = (bf16[5,64,128]{2,1,0:T(8,128)(2,1)S(1)}, bf16[5,64,128]{2,1,0:T(8,128)(2,1)S(1)}, u32[]{:S(2)}, u32[]{:S(2)}) collective-permute-start(bf16[5,64,128]{2,1,0:T(8,128)(2,1)S(1)} %get-tuple-element.32.refs_2_), channel_id=1, source_target_pairs={{0,4},{2,6},{4,8},{6,10},{8,12},{10,14},{12,0},{14,2},{1,5},{3,7},... | collective-permute-start | bytes 245768 | tf_op jit(solution)/shard_map/ppermute | solution.py:232
